TPU v7x, 32 devices: a whole 2x2x4 slice. The times are simulated.
32 devices in a mesh: grp: 2 (over x), tp: 16 (over z, y, core).
Axes of the slice: x: 2, y: 2, z: 4, core: 2. Of those that a mesh axis runs over, the one named last changes fastest.
Arguments:
- hidden_in: float32 [8, 4608], P('grp'), parts along dimension 0, may hold values from -6 to 6
- prefill_cache: bfloat16 [16, 1, 2, 4, 16, 8, 256], P('tp', None, None, 'grp'), parts along dimension 3, may hold values from -6 to 6
- lengths: int32 [8], P('grp'), parts along dimension 0, may hold values from 1 to 127
- page_table: int32 [8, 16], P('grp'), parts along dimension 0, may hold values from 0 to 15, each once within a row
- qkv_weight: bfloat16 [1, 8192, 4608], P(None, 'tp'), may hold values from -0.09375 to 0.09375
- out_weight: bfloat16 [1, 4608, 4096], P(None, 'tp'), may hold values from -0.09375 to 0.09375
- gate_up_weight: bfloat16 [1, 2, 18432, 4608], P(None, None, 'tp'), may hold values from -0.09375 to 0.09375
- down_weight: bfloat16 [1, 18432, 4608], P(None, 'tp'), may hold values from -0.0625 to 0.0625
- norm_gains: float32 [1, 4, 4608], replicated, may hold values from 0.25 to 1.75
Outputs:
- hidden_out: float32 [8, 4608], P('grp', 'tp'), parts along dimension 0
- decode_cache: bfloat16 [16, 1, 2, 8, 8, 2048], P('tp', None, None, 'grp'), parts along dimension 3
There are 2 independent parts, one for each index of `grp`. A program takes and returns all parts, laid end to end along the dimension named above; an argument that names none is the same for every part. Nothing has to cross between parts.
Inputs may be any that keep to these rules, and one draw needn't show every extreme that they name: Request r's new token takes position lengths[r]. Each row is a permutation of 0 to 15; page j of request r holds cache positions page_table[r, j] * 8 to page_table[r, j] * 8 + 7.
All inputs are finite; a program needn't handle non-finite values.
Results may differ from a plain program's by a relative error of at most 0.012.
The roundings to bfloat16 on the way count: a program that leaves them out, or rounds other values in their place, can miss the bound.
Values may be sent and summed in bfloat16 or wider, within the bound.
A program may use at most 128 MiB of HBM per device.

v0:
```python
import functools

import jax
import jax.numpy as jnp
from jax import lax
from jax.experimental import pallas as pl
from jax.experimental.pallas import tpu as pltpu
from jax.sharding import PartitionSpec as P

D = 4608
HEADS = 32
KV_HEADS = 16
HEAD_DIM = 128
PREFILL_TP = 8


EPSILON = 1e-06
SOFTCAP = 50.0


def rms_scale(vector, gain_row):
    meansq = jnp.mean(vector * vector, axis=-1, keepdims=True)
    return vector * lax.rsqrt(meansq + EPSILON) * (1.0 + gain_row)


def rotate(vector, positions):
    half_dim = vector.shape[-1] // 2
    exponent = jnp.arange(half_dim, dtype=jnp.float32) * (-2.0 / vector.shape[-1])
    frequency = jnp.power(jnp.float32(10000.0), exponent)
    angles = positions.astype(jnp.float32)[:, None, None] * frequency
    cosine = jnp.cos(angles)
    sine_term = jnp.sin(angles)
    front_half = vector[..., :half_dim]
    back_half = vector[..., half_dim:]
    return jnp.concatenate(
        [front_half * cosine - back_half * sine_term, back_half * cosine + front_half * sine_term],
        axis=-1,
    )


def capped(raw_scores):
    return SOFTCAP * jnp.tanh(raw_scores / SOFTCAP)


def round_back(vector):
    return lax.optimization_barrier(vector.astype(jnp.bfloat16)).astype(jnp.float32)


def pick_slot(vector, my_group, my_slot):
    inner = lax.dynamic_index_in_dim(vector, my_group, 0, False)
    return lax.dynamic_index_in_dim(inner, my_slot, 1, False)


def take_pages(page_block, page_order):
    return jnp.take(page_block, page_order, axis=2)


def project_rows(left, weight_rows):
    return jnp.einsum("bd,cd->bc", left, weight_rows, preferred_element_type=jnp.float32)


def on_device(
    hidden_in,
    prefill_cache,
    lengths,
    page_table,
    qkv_weight,
    out_weight,
    gate_up_weight,
    down_weight,
    norm_gains,
):
    devices = lax.axis_size("tp")
    my_index = lax.axis_index("tp")
    batch_rows = hidden_in.shape[0]
    groups = devices // PREFILL_TP
    per_group = batch_rows // groups
    local_heads = KV_HEADS // PREFILL_TP
    head_share = HEADS // KV_HEADS
    layer_count = prefill_cache.shape[1]
    page_width = prefill_cache.shape[5]
    score_scale = (D / HEADS) ** (-0.5)
    q_cols = HEADS * HEAD_DIM
    k_cols = KV_HEADS * HEAD_DIM
    my_group = my_index // PREFILL_TP
    my_slot = my_index % PREFILL_TP
    group_rows = lax.dynamic_slice_in_dim(page_table, my_group * per_group, per_group, 0)
    group_lengths = lax.dynamic_slice_in_dim(lengths, my_group * per_group, per_group, 0)
    local_cache = prefill_cache[0]
    page_ids = jnp.arange(devices, dtype=jnp.int32)
    onehot = (group_rows[:, :, None] == page_ids[None, None, :]).astype(jnp.int32)
    inverse = jnp.sum(onehot * page_ids[None, :, None], axis=1)
    arranged = jax.vmap(take_pages, in_axes=(2, 0), out_axes=2)(local_cache, inverse)
    relaid = lax.all_to_all(arranged, "tp", split_axis=3, concat_axis=3, tiled=True)
    relaid = relaid.reshape(
        layer_count, 2, per_group, groups, PREFILL_TP, page_width, local_heads, HEAD_DIM
    )
    decode_local = relaid.transpose(0, 1, 3, 2, 5, 4, 6, 7).reshape(
        layer_count, 2, batch_rows, page_width, k_cols
    )
    my_pos = my_index * page_width + jnp.arange(page_width, dtype=jnp.int32)
    fresh_slot = my_pos[None, :] == lengths[:, None]
    kept_cache = local_cache.reshape(
        layer_count, 2, per_group, devices, page_width, local_heads, HEAD_DIM
    )
    cache_pos = (
        group_rows[:, :, None] * page_width + jnp.arange(page_width, dtype=jnp.int32)[None, None, :]
    )
    kept_visible = cache_pos < group_lengths[:, None, None]
    stream = hidden_in
    normed = rms_scale(stream, norm_gains[0, 0]).astype(jnp.bfloat16)
    column_part = project_rows(normed, qkv_weight[0]).astype(jnp.bfloat16)
    projected = lax.all_gather(column_part, "tp", axis=1, tiled=True)
    queries = rotate(
        projected[:, :q_cols].astype(jnp.float32).reshape(batch_rows, HEADS, HEAD_DIM), lengths
    ).astype(jnp.bfloat16)
    new_key = rotate(
        projected[:, q_cols : q_cols + k_cols]
        .astype(jnp.float32)
        .reshape(batch_rows, KV_HEADS, HEAD_DIM),
        lengths,
    ).astype(jnp.bfloat16)
    new_value = projected[:, q_cols + k_cols :]
    key_layer = jnp.where(
        fresh_slot[:, :, None], new_key.reshape(batch_rows, 1, k_cols), decode_local[0, 0]
    )
    value_layer = jnp.where(
        fresh_slot[:, :, None], new_value.reshape(batch_rows, 1, k_cols), decode_local[0, 1]
    )
    written = [jnp.stack([key_layer, value_layer], axis=0)]
    flat_q = queries.reshape(batch_rows, KV_HEADS, head_share, HEAD_DIM)
    flat_k = new_key.reshape(batch_rows, KV_HEADS, 1, HEAD_DIM)
    flat_v = new_value.reshape(batch_rows, KV_HEADS, 1, HEAD_DIM)
    own_weight = jnp.exp(
        capped(
            jnp.sum(flat_q.astype(jnp.float32) * flat_k.astype(jnp.float32), axis=-1) * score_scale
        )
    )
    own_term = round_back(own_weight)[..., None] * flat_v.astype(jnp.float32)
    shaped_q = flat_q.reshape(groups, per_group, PREFILL_TP, local_heads, head_share, HEAD_DIM)
    shaped_own = own_weight.reshape(groups, per_group, PREFILL_TP, local_heads, head_share)
    shaped_term = own_term.reshape(groups, per_group, PREFILL_TP, local_heads, head_share, HEAD_DIM)
    my_queries = pick_slot(shaped_q, my_group, my_slot)
    cached_keys = kept_cache[0, 0]
    cached_values = kept_cache[0, 1]
    raw_scores = (
        jnp.einsum("ramd,rjcad->ramjc", my_queries, cached_keys, preferred_element_type=jnp.float32)
        * score_scale
    )
    weights = jnp.where(kept_visible[:, None, None, :, :], jnp.exp(capped(raw_scores)), 0.0)
    numerator = jnp.einsum(
        "ramjc,rjcad->ramd",
        weights.astype(jnp.bfloat16),
        cached_values,
        preferred_element_type=jnp.float32,
    )
    numerator = numerator + pick_slot(shaped_term, my_group, my_slot)
    denominator = jnp.sum(weights, axis=(-2, -1)) + pick_slot(shaped_own, my_group, my_slot)
    mine = (
        (numerator / denominator[..., None])
        .astype(jnp.bfloat16)
        .reshape(1, per_group, local_heads * head_share * HEAD_DIM)
    )
    gathered = lax.all_gather(mine, "tp", axis=0, tiled=True)
    attended = (
        gathered.reshape(groups, PREFILL_TP, per_group, local_heads * head_share * HEAD_DIM)
        .transpose(0, 2, 1, 3)
        .reshape(batch_rows, q_cols)
    )
    mixed_part = project_rows(attended, out_weight[0]).astype(jnp.bfloat16)
    mixed_out = lax.all_gather(mixed_part, "tp", axis=1, tiled=True)
    stream = stream + rms_scale(mixed_out.astype(jnp.float32), norm_gains[0, 1])
    ffn_in = rms_scale(stream, norm_gains[0, 2]).astype(jnp.bfloat16)
    gate_proj = project_rows(ffn_in, gate_up_weight[0, 0])
    up_proj = project_rows(ffn_in, gate_up_weight[0, 1])
    active = (jax.nn.gelu(gate_proj, approximate=True) * up_proj).astype(jnp.bfloat16)
    branch = jnp.dot(active, down_weight[0], preferred_element_type=jnp.float32)
    column_count = branch.shape[1] // devices
    summed = lax.psum(branch, "tp")
    stream = stream + rms_scale(summed, norm_gains[0, 3])
    result = lax.dynamic_slice_in_dim(stream, my_index * column_count, column_count, 1)
    decode_cache = jnp.stack(written, axis=0)[None]
    return (result, decode_cache)


MESH = pl.DeviceIdType.MESH
LANES = 128
NT = (((1,), (1,)), ((), ()))
LOG_BASE = 9.210340371976184
UNROLL = True
VMEM_LIMIT = 62 * 1024 * 1024


def dot_t(left, right):
    return lax.dot_general(left, right, NT, preferred_element_type=jnp.float32)


def normed_by(vector, meansq, gain):
    return vector * lax.rsqrt(meansq + EPSILON) * (1.0 + gain)


def meansq_of(vector):
    return jnp.mean(vector * vector, axis=-1, keepdims=True)


def column_of(scalars, count):
    row = lax.broadcasted_iota(jnp.int32, (count, 1), 0)
    column = jnp.zeros((count, 1), jnp.int32)
    for i in range(count):
        column = jnp.where(row == i, scalars[i], column)
    return column.astype(jnp.float32)


def fused_kernel(
    dims,
    len_ref,
    table_ref,
    hid_hbm,
    gain_hbm,
    flat_hbm,
    wq_hbm,
    wo_hbm,
    wgu_hbm,
    wd_hbm,
    out_ref,
    dec_hbm,
    hid,
    gain,
    table,
    flat,
    wq,
    wo,
    wgu,
    wd,
    proj,
    att,
    attended,
    mix,
    act,
    branch,
    stage,
    arrive,
    squares,
    page_stage,
    dec,
    dec_done,
    load_sem,
    send_sem,
    recv_sem,
):
    T, B, R, RP = dims["T"], dims["B"], dims["R"], dims["RP"]
    share, local_heads, slots = dims["share"], dims["local_heads"], dims["S"]
    per_group, groups = dims["per_group"], dims["groups"]
    width = local_heads * HEAD_DIM
    cols = wq.shape[0]
    heads_here = cols // HEAD_DIM
    q_devs = HEADS * HEAD_DIM // cols
    k_devs = KV_HEADS * HEAD_DIM // cols
    page_width = dec.shape[2]
    model = wq.shape[1]
    ff = wd.shape[0]
    chunks = model // LANES
    score_scale = (D / HEADS) ** (-0.5)
    me = lax.axis_index("tp")
    my_group = me // PREFILL_TP
    my_slot = me % PREFILL_TP

    def load(index, src, dst):
        return pltpu.make_async_copy(src, dst, load_sem.at[index])

    loads = [
        load(0, hid_hbm, hid.at[:, pl.ds(0, model)]),
        load(1, gain_hbm, gain.at[:, pl.ds(0, model)]),
        load(2, wq_hbm, wq),
        load(3, flat_hbm, flat),
        load(4, table_ref, table),
        load(5, wo_hbm, wo),
        load(6, wgu_hbm, wgu),
        load(7, wd_hbm, wd),
    ]
    for piece in loads[:5]:
        piece.start()

    barrier = pltpu.get_barrier_semaphore()

    def greet(step, carry):
        peer = lax.rem(me + step, T)
        pl.semaphore_signal(barrier, inc=1, device_id={"tp": peer}, device_id_type=MESH)
        return carry

    lax.fori_loop(1, T, greet, 0)

    def dec_part(ref, index):
        group, slot = index // PREFILL_TP, index % PREFILL_TP
        lane = pl.multiple_of(slot * width, width)
        return ref.at[:, pl.ds(group * per_group, per_group), :, pl.ds(lane, width)]

    def remote(which, src, dst, peer, sender):
        return pltpu.make_async_remote_copy(
            src_ref=src,
            dst_ref=dst,
            send_sem=send_sem.at[which, peer],
            recv_sem=recv_sem.at[which, sender],
            device_id={"tp": peer},
            device_id_type=MESH,
        )

    def owners(index):
        first = index % PREFILL_TP * local_heads
        key = first // heads_here
        return (first * share // heads_here, q_devs + key, q_devs + k_devs + key)

    def needs(receiver, sender):
        q_owner, k_owner, v_owner = owners(receiver)
        return (q_owner == sender) | (k_owner == sender) | (v_owner == sender)

    def each_projection(act_on, urgent, sending):
        for step in range(1, T):
            peer = lax.rem(me + step, T)
            hurry = needs(peer, me) if sending else needs(me, peer)

            @pl.when(hurry if urgent else jnp.logical_not(hurry))
            def _():
                act_on(peer)

    def send_projection(peer):
        remote(0, proj.at[me], proj.at[me], peer, me).start()

    def take_projection(peer):
        remote(0, proj.at[peer], proj.at[peer], peer, peer).wait_recv()

    def push_pages(begin, end):
        for step in range(begin, min(end, T)):
            peer = lax.rem(me + step, T)
            remote(3, page_stage.at[peer], dec_part(dec, me), peer, me).start()

    share_of = -(-(T - 1) // 4)

    def push(which, src_of, dst):
        def body(step, carry):
            peer = lax.rem(me + step, T)
            remote(which, src_of(peer), dst, peer, me).start()
            return carry

        lax.fori_loop(1, T, body, 0, unroll=UNROLL)

    def pull(which, src_of, dst_of):
        def body(step, carry):
            peer = lax.rem(me + step, T)
            remote(which, src_of(peer), dst_of(peer), peer, peer).wait_recv()
            return carry

        lax.fori_loop(1, T, body, 0, unroll=UNROLL)

    def drain(which, src_of, dst):
        def body(step, carry):
            peer = lax.rem(me + step, T)
            remote(which, src_of(peer), dst, peer, me).wait_send()
            return carry

        lax.fori_loop(1, T, body, 0, unroll=UNROLL)

    length = column_of(len_ref, B)
    lane = lax.broadcasted_iota(jnp.int32, (B, HEAD_DIM), 1)
    half = HEAD_DIM // 2
    exponent = (lane % half).astype(jnp.float32) * (-2.0 / HEAD_DIM)
    angles = length * jnp.exp(exponent * LOG_BASE)
    turning = jnp.broadcast_to(me < q_devs + k_devs, lane.shape)
    cosine = jnp.where(turning, jnp.cos(angles), 1.0)
    sine = jnp.where(turning, jnp.where(lane < half, -1.0, 1.0) * jnp.sin(angles), 0.0)
    loads[4].wait()
    slot_page = lax.broadcasted_iota(jnp.int32, (T, slots), 1) // page_width
    spread = (slot_page == lax.broadcasted_iota(jnp.int32, (T, slots), 0)).astype(jnp.float32)
    inside = lax.broadcasted_iota(jnp.int32, (B, slots), 1) % page_width
    position = jnp.dot(
        table[...].astype(jnp.float32).astype(jnp.bfloat16),
        spread.astype(jnp.bfloat16),
        preferred_element_type=jnp.float32,
    ) * page_width + inside.astype(jnp.float32)
    request_of = lax.broadcasted_iota(jnp.int32, (B, slots), 0)

    def row_at(values, request):
        return jnp.sum(jnp.where(request_of == request, values, 0.0), axis=0, keepdims=True)

    place = [row_at(position, my_group * per_group + e) for e in range(per_group)]
    limit = [
        row_at(jnp.broadcast_to(length, (B, slots)), my_group * per_group + e)
        for e in range(per_group)
    ]
    loads[0].wait()
    loads[1].wait()
    stream = hid[:, :model]
    normed = normed_by(stream, meansq_of(stream), gain[0:1, :model]).astype(jnp.bfloat16)
    loads[2].wait()
    for piece in loads[5:]:
        piece.start()
    part = dot_t(normed, wq[...]).astype(jnp.bfloat16).astype(jnp.float32)
    for head in range(heads_here):
        u = part[:, head * HEAD_DIM : (head + 1) * HEAD_DIM]
        swapped = jnp.concatenate([u[:, half:], u[:, :half]], axis=1)
        turned = u * cosine + swapped * sine
        proj[me, :, head * HEAD_DIM : (head + 1) * HEAD_DIM] = turned.astype(jnp.bfloat16)
    pl.semaphore_wait(barrier, T - 1)
    each_projection(send_projection, True, True)

    loads[3].wait()
    wanted = lax.broadcasted_iota(jnp.int32, (slots, slots), 0).astype(jnp.float32)
    for e in range(per_group):
        pick = (wanted == place[e]).astype(jnp.float32).astype(jnp.bfloat16)
        for c in range(2):
            moved = jnp.dot(pick, flat[c, e], preferred_element_type=jnp.float32)
            page_stage[:, c, e] = moved.reshape(T, page_width, width).astype(jnp.bfloat16)
    push_pages(1, 1 + share_of)
    each_projection(take_projection, True, False)

    rows = share * B
    row_of = lax.broadcasted_iota(jnp.int32, (rows, HEAD_DIM), 0)

    def head_of(first, index):
        owner = first + index // heads_here
        lane = pl.multiple_of((index % heads_here) * HEAD_DIM, HEAD_DIM)
        one = proj[owner, :, pl.ds(lane, HEAD_DIM)].astype(jnp.float32)
        return one

    for a in range(local_heads):
        kv_head = my_slot * local_heads + a
        q = jnp.concatenate([head_of(0, kv_head * share + m) for m in range(share)], axis=0)
        k_new = jnp.concatenate([head_of(q_devs, kv_head)] * share, axis=0)
        v_new = jnp.concatenate([head_of(q_devs + k_devs, kv_head)] * share, axis=0)
        q16 = q.astype(jnp.bfloat16)
        own = jnp.exp(capped(jnp.sum(q * k_new, axis=-1, keepdims=True) * score_scale))
        own_term = own.astype(jnp.bfloat16).astype(jnp.float32) * v_new
        lanes = slice(a * HEAD_DIM, (a + 1) * HEAD_DIM)
        found = [[] for m in range(share)]
        for e in range(per_group):
            request = my_group * per_group + e
            scores = dot_t(q16, flat[0, e, :, lanes]) * score_scale
            weights = jnp.where(place[e] < limit[e], jnp.exp(capped(scores)), 0.0)
            numer = jnp.dot(
                weights.astype(jnp.bfloat16),
                flat[1, e, :, lanes],
                preferred_element_type=jnp.float32,
            )
            denom = jnp.sum(weights, axis=-1, keepdims=True) + own
            result = (numer + own_term) / denom
            for m in range(share):
                chosen = jnp.where(row_of == m * B + request, result, 0.0)
                found[m].append(jnp.sum(chosen, axis=0, keepdims=True))
        for m in range(share):
            at = (a * share + m) * HEAD_DIM
            att[me, :, at : at + HEAD_DIM] = jnp.concatenate(found[m], axis=0).astype(jnp.bfloat16)
    push(1, lambda p: att.at[me], att.at[me])
    push_pages(1 + share_of, 1 + 2 * share_of)
    loads[5].wait()
    pull(1, lambda p: att.at[p], lambda p: att.at[p])
    q_width = att.shape[2]
    for s in range(PREFILL_TP):
        block = jnp.concatenate(
            [att[g * PREFILL_TP + s].astype(jnp.float32) for g in range(groups)], axis=0
        )
        attended[:, s * q_width : (s + 1) * q_width] = block.astype(jnp.bfloat16)
    mixed = dot_t(attended[...], wo[...]).astype(jnp.bfloat16)
    mix[me] = jnp.zeros((B, RP), jnp.bfloat16)
    mix[me, :, :R] = mixed
    push(2, lambda p: mix.at[me], mix.at[me])
    push_pages(1 + 2 * share_of, 1 + 3 * share_of)
    pull(2, lambda p: mix.at[p], lambda p: mix.at[p])

    gathered = [jnp.zeros((B, LANES), jnp.float32)] * chunks
    for s in range(T):
        first, shift = divmod(s * R, LANES)
        block = jnp.concatenate([mix[s].astype(jnp.float32), jnp.zeros((B, LANES), jnp.float32)], axis=1)
        if shift:
            block = pltpu.roll(block, shift, 1)
        for i in range(RP // LANES + 1):
            if first + i < chunks:
                gathered[first + i] = gathered[first + i] + block[:, i * LANES : (i + 1) * LANES]
    mixed_all = jnp.concatenate(gathered, axis=1)
    mixed_ms = meansq_of(mixed_all)
    stream = hid[:, :model] + normed_by(mixed_all, mixed_ms, gain[1:2, :model])
    ffn_in = normed_by(stream, meansq_of(stream), gain[2:3, :model]).astype(jnp.bfloat16)
    first_lane = pl.multiple_of(me * R // LANES * LANES, LANES)
    window = RP + LANES
    turn = window - lax.rem(me * R, LANES)
    own_hid = pltpu.roll(hid[:, pl.ds(first_lane, window)], turn, 1)[:, :RP]
    own_gain = pltpu.roll(gain[:, pl.ds(first_lane, window)], turn, 1)[:, :RP]
    mine = own_hid + normed_by(mix[me].astype(jnp.float32), mixed_ms, own_gain[1:2, :])

    push_pages(1 + 3 * share_of, T)
    each_projection(send_projection, False, True)
    dec_part(dec, me)[...] = page_stage[me]
    loads[6].wait()
    tile = dims["ff_tile"]

    def ffn(step, carry):
        at = pl.multiple_of(step * tile, tile)
        gate = dot_t(ffn_in, wgu[0, pl.ds(at, tile), :])
        up = dot_t(ffn_in, wgu[1, pl.ds(at, tile), :])
        act[:, pl.ds(at, tile)] = (jax.nn.gelu(gate, approximate=True) * up).astype(jnp.bfloat16)
        return carry

    lax.fori_loop(0, ff // tile, ffn, 0)
    loads[7].wait()
    active = act[...]
    out_tile = dims["out_tile"]

    def down(step, carry):
        at = pl.multiple_of(step * out_tile, out_tile)
        branch[:, pl.ds(at, out_tile)] = jnp.dot(
            active, wd[:, pl.ds(at, out_tile)], preferred_element_type=jnp.float32
        )
        return carry

    lax.fori_loop(0, model // out_tile, down, 0)
    for s in range(T):
        first, shift = divmod(s * R, LANES)
        parts = [
            branch[:, (first + i) * LANES : (first + i + 1) * LANES]
            if first + i < chunks
            else jnp.zeros((B, LANES), jnp.float32)
            for i in range(RP // LANES + 1)
        ]
        block = jnp.concatenate(parts, axis=1)
        if shift:
            block = pltpu.roll(block, block.shape[1] - shift, 1)
        stage[s] = block[:, :RP].astype(jnp.bfloat16)
    push(4, lambda p: stage.at[p], arrive.at[me])
    arrive[me] = stage[me]

    pull(3, lambda p: page_stage.at[p], lambda p: dec_part(dec, p))
    each_projection(take_projection, False, False)
    token = lax.broadcasted_iota(jnp.int32, (page_width, cols), 0) + me * page_width
    for c in range(2):
        for i in range(k_devs):
            fresh = proj[q_devs + c * k_devs + i].astype(jnp.float32)
            for r in range(B):
                old = dec[c, r, :, i * cols : (i + 1) * cols].astype(jnp.float32)
                row = jnp.broadcast_to(fresh[r : r + 1, :], old.shape)
                new = jnp.where(token == len_ref[r], row, old)
                dec_done[c, r, :, i * cols : (i + 1) * cols] = new.astype(jnp.bfloat16)
    store = pltpu.make_async_copy(dec_done, dec_hbm, load_sem.at[8])
    store.start()

    pull(4, lambda p: stage.at[p], lambda p: arrive.at[p])
    summed = arrive[0].astype(jnp.float32)
    for s in range(1, T):
        summed = summed + arrive[s].astype(jnp.float32)
    lane_of = lax.broadcasted_iota(jnp.int32, (B, RP), 1)
    summed = jnp.where(lane_of < R, summed, 0.0)
    squares[me] = jnp.broadcast_to(jnp.sum(summed * summed, axis=-1, keepdims=True), (B, LANES))
    push(5, lambda p: squares.at[me], squares.at[me])
    for which, src_of in (
        (0, lambda p: proj.at[me]),
        (1, lambda p: att.at[me]),
        (2, lambda p: mix.at[me]),
        (4, lambda p: stage.at[p]),
    ):
        drain(which, src_of, src_of(me))
    drain(3, lambda p: page_stage.at[p], dec_part(dec, me))
    pull(5, lambda p: squares.at[p], lambda p: squares.at[p])
    sumsq = squares[0]
    for s in range(1, T):
        sumsq = sumsq + squares[s]
    branch_ms = sumsq[:, 0:1] * (1.0 / model)
    result = mine + normed_by(summed, branch_ms, own_gain[3:4, :])
    out_ref[...] = result[:, :R]
    drain(5, lambda p: squares.at[me], squares.at[me])
    store.wait()


def finish_kernel(out_ref, dec_ref, out_done, dec_done):
    out_done[...] = out_ref[...]
    dec_done[...] = dec_ref[...]


def fits_kernel(shapes, devices):
    batch_rows, model = shapes["hidden"]
    cols, rows, ff = shapes["qkv"], shapes["out"], shapes["ff"]
    groups = devices // PREFILL_TP
    weight_bytes = 2 * (cols * model + rows * HEADS * HEAD_DIM + 3 * ff * model)
    return (
        cols == HEADS // PREFILL_TP * HEAD_DIM
        and (KV_HEADS * HEAD_DIM) % cols == 0
        and (HEADS * HEAD_DIM) % cols == 0
        and batch_rows % groups == 0
        and model % LANES == 0
        and ff % LANES == 0
        and rows * devices == model
        and weight_bytes < VMEM_LIMIT * 3 // 4
        and batch_rows <= 8
    )


def largest_tile(total, limit):
    return max(t for t in range(LANES, limit + 1, LANES) if total % t == 0)


def fused_device(
    hidden_in,
    prefill_cache,
    lengths,
    page_table,
    qkv_weight,
    out_weight,
    gate_up_weight,
    down_weight,
    norm_gains,
):
    T = lax.axis_size("tp")
    B, model = hidden_in.shape
    groups = T // PREFILL_TP
    per_group = B // groups
    local_heads = KV_HEADS // PREFILL_TP
    share = HEADS // KV_HEADS
    pages, page_width, width = prefill_cache.shape[4:]
    S = pages * page_width
    cols = qkv_weight.shape[1]
    R = out_weight.shape[1]
    RP = -(-R // LANES) * LANES
    ff = down_weight.shape[1]
    k_cols = KV_HEADS * HEAD_DIM
    dims = dict(
        T=T, B=B, R=R, RP=RP, S=S, share=share, local_heads=local_heads,
        per_group=per_group, groups=groups,
        ff_tile=largest_tile(ff, 384), out_tile=largest_tile(model, 512),
    )
    q_width = local_heads * share * HEAD_DIM
    bf16, f32 = jnp.bfloat16, jnp.float32
    smem = pl.BlockSpec(memory_space=pltpu.SMEM)
    vmem = pl.BlockSpec(memory_space=pltpu.VMEM)
    anyw = pl.BlockSpec(memory_space=pl.ANY)
    out, dec = pl.pallas_call(
        functools.partial(fused_kernel, dims),
        out_shape=(
            jax.ShapeDtypeStruct((B, R), f32),
            jax.ShapeDtypeStruct((2, B, page_width, k_cols), bf16),
        ),
        in_specs=[smem] + [anyw] * 8,
        out_specs=(vmem, anyw),
        scratch_shapes=[
            pltpu.VMEM((B, model + RP), f32),
            pltpu.VMEM((norm_gains.shape[1], model + RP), f32),
            pltpu.VMEM((B, T), jnp.int32),
            pltpu.VMEM((2, per_group, S, width), bf16),
            pltpu.VMEM((cols, model), bf16),
            pltpu.VMEM((R, HEADS * HEAD_DIM), bf16),
            pltpu.VMEM((2, ff, model), bf16),
            pltpu.VMEM((ff, model), bf16),
            pltpu.VMEM((T, B, cols), bf16),
            pltpu.VMEM((T, per_group, q_width), bf16),
            pltpu.VMEM((B, HEADS * HEAD_DIM), bf16),
            pltpu.VMEM((T, B, RP), bf16),
            pltpu.VMEM((B, ff), bf16),
            pltpu.VMEM((B, model), f32),
            pltpu.VMEM((T, B, RP), bf16),
            pltpu.VMEM((T, B, RP), bf16),
            pltpu.VMEM((T, B, LANES), f32),
            pltpu.VMEM((T, 2, per_group, page_width, width), bf16),
            pltpu.VMEM((2, B, page_width, k_cols), bf16),
            pltpu.VMEM((2, B, page_width, k_cols), bf16),
            pltpu.SemaphoreType.DMA((9,)),
            pltpu.SemaphoreType.DMA((6, T)),
            pltpu.SemaphoreType.DMA((6, T)),
        ],
        compiler_params=pltpu.CompilerParams(
            collective_id=0, has_side_effects=True, vmem_limit_bytes=VMEM_LIMIT
        ),
    )(
        lengths,
        page_table,
        hidden_in,
        norm_gains[0],
        prefill_cache.reshape(2, per_group, S, width),
        qkv_weight[0],
        out_weight[0],
        gate_up_weight[0],
        down_weight[0],
    )
    out, dec = pl.pallas_call(
        finish_kernel,
        out_shape=(
            jax.ShapeDtypeStruct(out.shape, f32),
            jax.ShapeDtypeStruct(dec.shape, bf16),
        ),
        in_specs=[vmem, vmem],
        out_specs=(vmem, vmem),
    )(out, dec)
    return out, dec.reshape(1, 1, 2, B, page_width, k_cols)


def step(*args):
    shapes = {
        "hidden": args[0].shape,
        "qkv": args[4].shape[1],
        "out": args[5].shape[1],
        "ff": args[7].shape[1],
    }
    chosen = fused_device if fits_kernel(shapes, lax.axis_size("tp")) else on_device
    return chosen(*args)


def solution(mesh):
    placed = (
        P("grp", None),
        P("tp", None, None, "grp", None, None, None),
        P("grp"),
        P("grp", None),
        P(None, "tp", None),
        P(None, "tp", None),
        P(None, None, "tp", None),
        P(None, "tp", None),
        P(),
    )
    return jax.shard_map(
        step,
        mesh=mesh,
        in_specs=placed,
        out_specs=(P("grp", "tp"), P("tp", None, None, "grp", None, None)),
        check_vma=False,
    )
```

profile of v0, /device:TPU:0, one launch (start us, length us, event | category | flops | bytes accessed | tf_op | source)
XLA Modules:
  0.0 44.2 jit_solution(1405805260999965179)
XLA Ops:
  0.6 41.9 %shard_map.104 = (f32[4,288]{1,0:T(4,128)}, bf16[2,4,8,2048]{3,2,1,0:T(8,128)(2,1)}) custom-call(s32[4]{0:T(128)} %len_ref.1, s32[4,16]{1,0:T(4,128)} %table_ref.1, f32[4,4608]{1,0:T(4,128)} %hid_hbm.1, f32[4,4608]{1,0:T(4,128)} %bitcast.12, bf16[2,2,128,256]{3,2,1,0:T(8,128)(2,1)} %bitcast.11, bf16[512,4608]{1,0:T(8,128)(2,1)} %bitcast.9, ...), custom_call_target="tpu_custom_call" | custom-call | tf_op jit(solution)/shard_map/pallas_call | solution.py:632
  42.6 1.7 %shard_map.105 = (f32[4,288]{1,0:T(4,128)}, bf16[2,4,8,2048]{3,2,1,0:T(8,128)(2,1)}) custom-call(f32[4,288]{1,0:T(4,128)} %get-tuple-element.6.out_ref, bf16[2,4,8,2048]{3,2,1,0:T(8,128)(2,1)} %get-tuple-element.7.dec_ref), custom_call_target="tpu_custom_call" | custom-call | tf_op jit(solution)/shard_map/pallas_call | solution.py:679
where the time goes:
time: 44.5 us; the launch traced here: 44.2 us
  Pallas kernels  43.6 us (98%)
  between operations  0.64 us (1%)
    pallas_call x1, Pallas kernels, fused_device(): pl.pallas_call(functools.partial(fused_kernel, dims), out_shape=(jax.Shap...  41.9 us
    pallas_call x1, Pallas kernels, fused_device(): pl.pallas_call(finish_kernel, out_shape=(jax.ShapeDtypeStruct(out.shape,...  1.69 us

commit v1 on v0

--- a/solution.py
+++ b/solution.py
@@ -188,7 +188,7 @@
 NT = (((1,), (1,)), ((), ()))
 LOG_BASE = 9.210340371976184
 UNROLL = True
-VMEM_LIMIT = 62 * 1024 * 1024
+VMEM_LIMIT = 58 * 1024 * 1024
 
 
 def dot_t(left, right):
@@ -211,10 +211,16 @@
     return column.astype(jnp.float32)
 
 
+def pad_rows(rows, count):
+    return jnp.concatenate(
+        [rows, jnp.zeros((count - rows.shape[0], rows.shape[1]), rows.dtype)], axis=0
+    )
+
+
 def fused_kernel(
     dims,
-    len_ref,
-    table_ref,
+    len_hbm,
+    table_hbm,
     hid_hbm,
     gain_hbm,
     flat_hbm,
@@ -223,7 +229,8 @@
     wgu_hbm,
     wd_hbm,
     out_ref,
-    dec_hbm,
+    dec_done,
+    len_ref,
     hid,
     gain,
     table,
@@ -236,21 +243,25 @@
     att,
     attended,
     mix,
-    act,
     branch,
-    stage,
     arrive,
+    sums,
     squares,
+    turned_act,
     page_stage,
     dec,
-    dec_done,
     load_sem,
     send_sem,
-    recv_sem,
+    proj_sem,
+    att_sem,
+    mix_sem,
+    tail_sem,
 ):
     T, B, R, RP = dims["T"], dims["B"], dims["R"], dims["RP"]
     share, local_heads, slots = dims["share"], dims["local_heads"], dims["S"]
     per_group, groups = dims["per_group"], dims["groups"]
+    planes, plane_size = dims["planes"], dims["plane_size"]
+    first_owner, owner_count = dims["first_owner"], dims["owner_count"]
     width = local_heads * HEAD_DIM
     cols = wq.shape[0]
     heads_here = cols // HEAD_DIM
@@ -264,21 +275,28 @@
     me = lax.axis_index("tp")
     my_group = me // PREFILL_TP
     my_slot = me % PREFILL_TP
+    my_plane = me // plane_size
+    my_seat = me % plane_size
 
     def load(index, src, dst):
         return pltpu.make_async_copy(src, dst, load_sem.at[index])
 
-    loads = [
+    small = [
         load(0, hid_hbm, hid.at[:, pl.ds(0, model)]),
         load(1, gain_hbm, gain.at[:, pl.ds(0, model)]),
-        load(2, wq_hbm, wq),
-        load(3, flat_hbm, flat),
-        load(4, table_ref, table),
-        load(5, wo_hbm, wo),
-        load(6, wgu_hbm, wgu),
-        load(7, wd_hbm, wd),
+        load(2, len_hbm, len_ref),
+        load(3, table_hbm, table),
     ]
-    for piece in loads[:5]:
+    cuts = dims["cuts"]
+    wq_loads = [
+        load(8 + i, wq_hbm.at[:, pl.ds(lo, hi - lo)], wq.at[:, pl.ds(lo, hi - lo)])
+        for i, (lo, hi) in enumerate(cuts)
+    ]
+    flat_load = load(4, flat_hbm, flat)
+    wo_load = load(5, wo_hbm, wo)
+    wgu_load = load(6, wgu_hbm, wgu)
+    wd_load = load(7, wd_hbm, wd)
+    for piece in small + wq_loads + [flat_load]:
         piece.start()
 
     barrier = pltpu.get_barrier_semaphore()
@@ -295,71 +313,73 @@
         lane = pl.multiple_of(slot * width, width)
         return ref.at[:, pl.ds(group * per_group, per_group), :, pl.ds(lane, width)]
 
-    def remote(which, src, dst, peer, sender):
+    def remote(src, dst, send, recv, peer):
         return pltpu.make_async_remote_copy(
             src_ref=src,
             dst_ref=dst,
-            send_sem=send_sem.at[which, peer],
-            recv_sem=recv_sem.at[which, sender],
+            send_sem=send_sem.at[send],
+            recv_sem=recv,
             device_id={"tp": peer},
             device_id_type=MESH,
         )
+
+    def sent(send, ref):
+        remote(ref, ref, send, tail_sem.at[0], me).wait_send()
+
+    def landed(recv, ref):
+        remote(ref, ref, 0, recv, me).wait_recv()
 
     def owners(index):
         first = index % PREFILL_TP * local_heads
         key = first // heads_here
         return (first * share // heads_here, q_devs + key, q_devs + k_devs + key)
 
-    def needs(receiver, sender):
-        q_owner, k_owner, v_owner = owners(receiver)
-        return (q_owner == sender) | (k_owner == sender) | (v_owner == sender)
-
-    def each_projection(act_on, urgent, sending):
+    def proj_from(sender):
+        return proj_sem.at[jnp.maximum(sender - (q_devs - 1), 0)]
+
+    def send_proj(peer):
+        remote(proj.at[me], proj.at[me], 0, proj_from(me), peer).start()
+
+    def send_projections(urgent):
         for step in range(1, T):
             peer = lax.rem(me + step, T)
-            hurry = needs(peer, me) if sending else needs(me, peer)
-
-            @pl.when(hurry if urgent else jnp.logical_not(hurry))
+            q_owner, k_owner, v_owner = owners(peer)
+            hurry = (q_owner == me) | (k_owner == me) | (v_owner == me)
+            wanted = hurry if urgent else jnp.logical_not(hurry) & (me >= q_devs)
+
+            @pl.when(wanted)
             def _():
-                act_on(peer)
-
-    def send_projection(peer):
-        remote(0, proj.at[me], proj.at[me], peer, me).start()
-
-    def take_projection(peer):
-        remote(0, proj.at[peer], proj.at[peer], peer, peer).wait_recv()
+                send_proj(peer)
+
+    def take_proj(sender):
+        @pl.when(sender != me)
+        def _():
+            landed(proj_from(sender), proj.at[sender])
 
     def push_pages(begin, end):
         for step in range(begin, min(end, T)):
             peer = lax.rem(me + step, T)
-            remote(3, page_stage.at[peer], dec_part(dec, me), peer, me).start()
+            remote(page_stage.at[peer], dec_part(dec, me), 1, tail_sem.at[3], peer).start()
 
     share_of = -(-(T - 1) // 4)
 
-    def push(which, src_of, dst):
-        def body(step, carry):
+    def push(send, recv, src):
+        for step in range(1, T):
             peer = lax.rem(me + step, T)
-            remote(which, src_of(peer), dst, peer, me).start()
-            return carry
-
-        lax.fori_loop(1, T, body, 0, unroll=UNROLL)
-
-    def pull(which, src_of, dst_of):
-        def body(step, carry):
-            peer = lax.rem(me + step, T)
-            remote(which, src_of(peer), dst_of(peer), peer, peer).wait_recv()
-            return carry
-
-        lax.fori_loop(1, T, body, 0, unroll=UNROLL)
-
-    def drain(which, src_of, dst):
-        def body(step, carry):
-            peer = lax.rem(me + step, T)
-            remote(which, src_of(peer), dst, peer, me).wait_send()
-            return carry
-
-        lax.fori_loop(1, T, body, 0, unroll=UNROLL)
-
+            remote(src, src, send, recv, peer).start()
+
+    def take_plane(sems, ref, plane):
+        first = plane * plane_size
+
+        @pl.when(plane == my_plane)
+        def _():
+            landed(sems.at[plane], ref.at[pl.ds(first, plane_size - 1)])
+
+        @pl.when(plane != my_plane)
+        def _():
+            landed(sems.at[plane], ref.at[pl.ds(first, plane_size)])
+
+    small[2].wait()
     length = column_of(len_ref, B)
     lane = lax.broadcasted_iota(jnp.int32, (B, HEAD_DIM), 1)
     half = HEAD_DIM // 2
@@ -368,7 +388,7 @@
     turning = jnp.broadcast_to(me < q_devs + k_devs, lane.shape)
     cosine = jnp.where(turning, jnp.cos(angles), 1.0)
     sine = jnp.where(turning, jnp.where(lane < half, -1.0, 1.0) * jnp.sin(angles), 0.0)
-    loads[4].wait()
+    small[3].wait()
     slot_page = lax.broadcasted_iota(jnp.int32, (T, slots), 1) // page_width
     spread = (slot_page == lax.broadcasted_iota(jnp.int32, (T, slots), 0)).astype(jnp.float32)
     inside = lax.broadcasted_iota(jnp.int32, (B, slots), 1) % page_width
@@ -387,23 +407,27 @@
         row_at(jnp.broadcast_to(length, (B, slots)), my_group * per_group + e)
         for e in range(per_group)
     ]
-    loads[0].wait()
-    loads[1].wait()
+    small[0].wait()
+    small[1].wait()
     stream = hid[:, :model]
     normed = normed_by(stream, meansq_of(stream), gain[0:1, :model]).astype(jnp.bfloat16)
-    loads[2].wait()
-    for piece in loads[5:]:
-        piece.start()
-    part = dot_t(normed, wq[...]).astype(jnp.bfloat16).astype(jnp.float32)
+    part = jnp.zeros((B, cols), jnp.float32)
+    for (lo, hi), piece in zip(cuts, wq_loads):
+        piece.wait()
+        if hi == model:
+            for late in (wo_load, wgu_load, wd_load):
+                late.start()
+        part = part + dot_t(normed[:, lo:hi], wq[:, lo:hi])
+    part = part.astype(jnp.bfloat16).astype(jnp.float32)
     for head in range(heads_here):
         u = part[:, head * HEAD_DIM : (head + 1) * HEAD_DIM]
         swapped = jnp.concatenate([u[:, half:], u[:, :half]], axis=1)
         turned = u * cosine + swapped * sine
         proj[me, :, head * HEAD_DIM : (head + 1) * HEAD_DIM] = turned.astype(jnp.bfloat16)
     pl.semaphore_wait(barrier, T - 1)
-    each_projection(send_projection, True, True)
-
-    loads[3].wait()
+    send_projections(True)
+
+    flat_load.wait()
     wanted = lax.broadcasted_iota(jnp.int32, (slots, slots), 0).astype(jnp.float32)
     for e in range(per_group):
         pick = (wanted == place[e]).astype(jnp.float32).astype(jnp.bfloat16)
@@ -411,29 +435,26 @@
             moved = jnp.dot(pick, flat[c, e], preferred_element_type=jnp.float32)
             page_stage[:, c, e] = moved.reshape(T, page_width, width).astype(jnp.bfloat16)
     push_pages(1, 1 + share_of)
-    each_projection(take_projection, True, False)
+    q_from, k_from, v_from = owners(me)
+    take_proj(q_from)
+    take_proj(k_from)
 
     rows = share * B
     row_of = lax.broadcasted_iota(jnp.int32, (rows, HEAD_DIM), 0)
 
-    def head_of(first, index):
-        owner = first + index // heads_here
-        lane = pl.multiple_of((index % heads_here) * HEAD_DIM, HEAD_DIM)
-        one = proj[owner, :, pl.ds(lane, HEAD_DIM)].astype(jnp.float32)
-        return one
-
+    def head_of(owner, index):
+        at = pl.multiple_of((index % heads_here) * HEAD_DIM, HEAD_DIM)
+        return proj[owner, :, pl.ds(at, HEAD_DIM)].astype(jnp.float32)
+
+    found = {}
     for a in range(local_heads):
         kv_head = my_slot * local_heads + a
-        q = jnp.concatenate([head_of(0, kv_head * share + m) for m in range(share)], axis=0)
-        k_new = jnp.concatenate([head_of(q_devs, kv_head)] * share, axis=0)
-        v_new = jnp.concatenate([head_of(q_devs + k_devs, kv_head)] * share, axis=0)
+        q = jnp.concatenate([head_of(q_from, kv_head * share + m) for m in range(share)], axis=0)
+        k_new = jnp.concatenate([head_of(k_from, kv_head)] * share, axis=0)
         q16 = q.astype(jnp.bfloat16)
         own = jnp.exp(capped(jnp.sum(q * k_new, axis=-1, keepdims=True) * score_scale))
-        own_term = own.astype(jnp.bfloat16).astype(jnp.float32) * v_new
         lanes = slice(a * HEAD_DIM, (a + 1) * HEAD_DIM)
-        found = [[] for m in range(share)]
         for e in range(per_group):
-            request = my_group * per_group + e
             scores = dot_t(q16, flat[0, e, :, lanes]) * score_scale
             weights = jnp.where(place[e] < limit[e], jnp.exp(capped(scores)), 0.0)
             numer = jnp.dot(
@@ -441,94 +462,121 @@
                 flat[1, e, :, lanes],
                 preferred_element_type=jnp.float32,
             )
-            denom = jnp.sum(weights, axis=-1, keepdims=True) + own
-            result = (numer + own_term) / denom
+            found[a, e] = (numer, jnp.sum(weights, axis=-1, keepdims=True) + own, own)
+    take_proj(v_from)
+    for a in range(local_heads):
+        kv_head = my_slot * local_heads + a
+        v_new = jnp.concatenate([head_of(v_from, kv_head)] * share, axis=0)
+        picked = [[] for m in range(share)]
+        for e in range(per_group):
+            request = my_group * per_group + e
+            numer, denom, own = found[a, e]
+            result = (numer + own.astype(jnp.bfloat16).astype(jnp.float32) * v_new) / denom
             for m in range(share):
                 chosen = jnp.where(row_of == m * B + request, result, 0.0)
-                found[m].append(jnp.sum(chosen, axis=0, keepdims=True))
+                picked[m].append(jnp.sum(chosen, axis=0, keepdims=True))
         for m in range(share):
             at = (a * share + m) * HEAD_DIM
-            att[me, :, at : at + HEAD_DIM] = jnp.concatenate(found[m], axis=0).astype(jnp.bfloat16)
-    push(1, lambda p: att.at[me], att.at[me])
+            att[me, :, at : at + HEAD_DIM] = jnp.concatenate(picked[m], axis=0).astype(jnp.bfloat16)
+    push(2, att_sem.at[my_plane], att.at[me])
     push_pages(1 + share_of, 1 + 2 * share_of)
-    loads[5].wait()
-    pull(1, lambda p: att.at[p], lambda p: att.at[p])
-    q_width = att.shape[2]
-    for s in range(PREFILL_TP):
-        block = jnp.concatenate(
-            [att[g * PREFILL_TP + s].astype(jnp.float32) for g in range(groups)], axis=0
-        )
-        attended[:, s * q_width : (s + 1) * q_width] = block.astype(jnp.bfloat16)
-    mixed = dot_t(attended[...], wo[...]).astype(jnp.bfloat16)
-    mix[me] = jnp.zeros((B, RP), jnp.bfloat16)
-    mix[me, :, :R] = mixed
-    push(2, lambda p: mix.at[me], mix.at[me])
-    push_pages(1 + 2 * share_of, 1 + 3 * share_of)
-    pull(2, lambda p: mix.at[p], lambda p: mix.at[p])
-
-    gathered = [jnp.zeros((B, LANES), jnp.float32)] * chunks
-    for s in range(T):
-        first, shift = divmod(s * R, LANES)
-        block = jnp.concatenate([mix[s].astype(jnp.float32), jnp.zeros((B, LANES), jnp.float32)], axis=1)
-        if shift:
-            block = pltpu.roll(block, shift, 1)
-        for i in range(RP // LANES + 1):
-            if first + i < chunks:
-                gathered[first + i] = gathered[first + i] + block[:, i * LANES : (i + 1) * LANES]
-    mixed_all = jnp.concatenate(gathered, axis=1)
-    mixed_ms = meansq_of(mixed_all)
-    stream = hid[:, :model] + normed_by(mixed_all, mixed_ms, gain[1:2, :model])
-    ffn_in = normed_by(stream, meansq_of(stream), gain[2:3, :model]).astype(jnp.bfloat16)
+
     first_lane = pl.multiple_of(me * R // LANES * LANES, LANES)
     window = RP + LANES
     turn = window - lax.rem(me * R, LANES)
     own_hid = pltpu.roll(hid[:, pl.ds(first_lane, window)], turn, 1)[:, :RP]
     own_gain = pltpu.roll(gain[:, pl.ds(first_lane, window)], turn, 1)[:, :RP]
-    mine = own_hid + normed_by(mix[me].astype(jnp.float32), mixed_ms, own_gain[1:2, :])
+    wo_load.wait()
+    q_width = att.shape[2]
+    halves = T // PREFILL_TP
+    slots_half = PREFILL_TP // halves
+    half_width = slots_half * q_width
+    mixed = jnp.zeros((B, R), jnp.float32)
+    for turn_of in range(halves):
+        which = (my_plane // (planes // halves) + turn_of) % halves
+        for g in range(groups):
+            take_plane(att_sem, att, g * halves + which)
+        blocks = [
+            jnp.concatenate(
+                [
+                    att[g * PREFILL_TP + which * slots_half + s].astype(jnp.float32)
+                    for g in range(groups)
+                ],
+                axis=0,
+            ).astype(jnp.bfloat16)
+            for s in range(slots_half)
+        ]
+        lane_at = pl.multiple_of(which * half_width, half_width)
+        mixed = mixed + dot_t(
+            jnp.concatenate(blocks, axis=1), wo[:, pl.ds(lane_at, half_width)]
+        )
+    mixed = mixed.astype(jnp.bfloat16).astype(jnp.float32)
+    mixed = jnp.concatenate([mixed, jnp.zeros((B, RP - R), jnp.float32)], axis=1)
+    shift = dims["seat_shift"]
+    mix[me] = pltpu.roll(mixed, my_seat * shift, 1).astype(jnp.bfloat16)
+    push(3, mix_sem.at[my_plane], mix.at[me])
+    push_pages(1 + 2 * share_of, 1 + 3 * share_of)
+    for step in range(planes):
+        take_plane(mix_sem, mix, jnp.int32(step))
+
+    gathered = [None] * chunks
+    for s in range(T):
+        block = mix[s].astype(jnp.float32)
+        for i in range(RP // LANES):
+            at = s * R // LANES + i
+            tile = block[:, i * LANES : (i + 1) * LANES]
+            if at < chunks:
+                gathered[at] = tile if gathered[at] is None else gathered[at] + tile
+    mixed_all = jnp.concatenate(gathered, axis=1)
+    mixed_ms = meansq_of(mixed_all)
+    stream = hid[:, :model] + normed_by(mixed_all, mixed_ms, gain[1:2, :model])
+    ffn_in = normed_by(stream, meansq_of(stream), gain[2:3, :model]).astype(jnp.bfloat16)
+    mine = own_hid + normed_by(mixed, mixed_ms, own_gain[1:2, :])
 
     push_pages(1 + 3 * share_of, T)
-    each_projection(send_projection, False, True)
+    wgu_load.wait()
+    side = ff // 2
+    tile = dims["ff_tile"]
+    probe = pad_rows(ffn_in, SUBLANES)
+    fronts = []
+    at_lane = tile // LANES * LANES
+    for at in range(0, side, tile):
+        flatwise = []
+        upright = []
+        for c in range(2):
+            pushed = jnp.concatenate([wgu[c, at : at + tile, :], probe], axis=0)
+            passed = jnp.concatenate([probe, wgu[c, side + at : side + at + tile, :]], axis=0)
+            both = dot_t(passed, pushed)
+            flatwise.append(both[:B, :tile])
+            upright.append(both[SUBLANES:, at_lane:])
+        fronts.append(jax.nn.gelu(flatwise[0], approximate=True) * flatwise[1])
+        turned_act[at : at + tile, : upright[0].shape[1]] = (
+            jax.nn.gelu(upright[0], approximate=True) * upright[1]
+        )
+    back = turned_act[...].T[tile - at_lane : tile - at_lane + B, :side]
+    active = jnp.concatenate(fronts + [back], axis=1).astype(jnp.bfloat16)
+    wd_load.wait()
+    branch[...] = jnp.dot(active, wd[...], preferred_element_type=jnp.float32).astype(jnp.bfloat16)
+
+    owned = model // owner_count
+    span = arrive.shape[2]
+    is_owner = (me >= first_owner) & (me < first_owner + owner_count)
+    for o in range(owner_count):
+        peer = first_owner + o
+
+        @pl.when(me != peer)
+        def _():
+            piece = branch.at[:, pl.ds(o * owned // LANES * LANES, span)]
+            remote(piece, arrive.at[me], 4, tail_sem.at[0], jnp.int32(peer)).start()
+
+    send_projections(False)
     dec_part(dec, me)[...] = page_stage[me]
-    loads[6].wait()
-    tile = dims["ff_tile"]
-
-    def ffn(step, carry):
-        at = pl.multiple_of(step * tile, tile)
-        gate = dot_t(ffn_in, wgu[0, pl.ds(at, tile), :])
-        up = dot_t(ffn_in, wgu[1, pl.ds(at, tile), :])
-        act[:, pl.ds(at, tile)] = (jax.nn.gelu(gate, approximate=True) * up).astype(jnp.bfloat16)
-        return carry
-
-    lax.fori_loop(0, ff // tile, ffn, 0)
-    loads[7].wait()
-    active = act[...]
-    out_tile = dims["out_tile"]
-
-    def down(step, carry):
-        at = pl.multiple_of(step * out_tile, out_tile)
-        branch[:, pl.ds(at, out_tile)] = jnp.dot(
-            active, wd[:, pl.ds(at, out_tile)], preferred_element_type=jnp.float32
-        )
-        return carry
-
-    lax.fori_loop(0, model // out_tile, down, 0)
-    for s in range(T):
-        first, shift = divmod(s * R, LANES)
-        parts = [
-            branch[:, (first + i) * LANES : (first + i + 1) * LANES]
-            if first + i < chunks
-            else jnp.zeros((B, LANES), jnp.float32)
-            for i in range(RP // LANES + 1)
-        ]
-        block = jnp.concatenate(parts, axis=1)
-        if shift:
-            block = pltpu.roll(block, block.shape[1] - shift, 1)
-        stage[s] = block[:, :RP].astype(jnp.bfloat16)
-    push(4, lambda p: stage.at[p], arrive.at[me])
-    arrive[me] = stage[me]
-
-    pull(3, lambda p: page_stage.at[p], lambda p: dec_part(dec, p))
-    each_projection(take_projection, False, False)
+    landed(tail_sem.at[3], page_stage.at[pl.ds(0, T - 1)])
+    for owner in range(q_devs, q_devs + 2 * k_devs):
+        @pl.when((owner != k_from) & (owner != v_from))
+        def _():
+            take_proj(jnp.int32(owner))
+
     token = lax.broadcasted_iota(jnp.int32, (page_width, cols), 0) + me * page_width
     for c in range(2):
         for i in range(k_devs):
@@ -538,39 +586,112 @@
                 row = jnp.broadcast_to(fresh[r : r + 1, :], old.shape)
                 new = jnp.where(token == len_ref[r], row, old)
                 dec_done[c, r, :, i * cols : (i + 1) * cols] = new.astype(jnp.bfloat16)
-    store = pltpu.make_async_copy(dec_done, dec_hbm, load_sem.at[8])
-    store.start()
-
-    pull(4, lambda p: stage.at[p], lambda p: arrive.at[p])
-    summed = arrive[0].astype(jnp.float32)
-    for s in range(1, T):
-        summed = summed + arrive[s].astype(jnp.float32)
-    lane_of = lax.broadcasted_iota(jnp.int32, (B, RP), 1)
-    summed = jnp.where(lane_of < R, summed, 0.0)
-    squares[me] = jnp.broadcast_to(jnp.sum(summed * summed, axis=-1, keepdims=True), (B, LANES))
-    push(5, lambda p: squares.at[me], squares.at[me])
-    for which, src_of in (
-        (0, lambda p: proj.at[me]),
-        (1, lambda p: att.at[me]),
-        (2, lambda p: mix.at[me]),
-        (4, lambda p: stage.at[p]),
-    ):
-        drain(which, src_of, src_of(me))
-    drain(3, lambda p: page_stage.at[p], dec_part(dec, me))
-    pull(5, lambda p: squares.at[p], lambda p: squares.at[p])
+
+    @pl.when(is_owner)
+    def _():
+        o = me - first_owner
+        odd = o % 2
+        base = pl.multiple_of(o * owned // LANES * LANES, LANES)
+        total = branch[:, pl.ds(base, span)].astype(jnp.float32)
+        landed(tail_sem.at[0], arrive.at[pl.ds(0, T - 1)])
+        for s in range(T):
+            piece = arrive[s].astype(jnp.float32)
+            total = total + jnp.where(me == s, 0.0, piece)
+        offset = odd * (LANES // 2)
+        lane_of = lax.broadcasted_iota(jnp.int32, (B, span), 1)
+        inside = (lane_of >= offset) & (lane_of < offset + owned)
+        kept = jnp.where(inside, total, 0.0)
+        ready = []
+        for i in range(2):
+            begin = i * R // LANES * LANES
+            left = RP - (i * R - begin) - offset
+            ready.append(pltpu.roll(kept[:, begin : begin + RP], lax.rem(left, RP), 1))
+            sums[i] = ready[i]
+        for i in range(2):
+            peer = o * 2 + i
+
+            @pl.when(peer != me)
+            def _():
+                remote(sums.at[i], sums.at[2], 5, tail_sem.at[1], peer).start()
+
+            @pl.when(peer == me)
+            def _():
+                sums[2] = ready[i]
+
+        each = jnp.sum(kept * kept, axis=-1, keepdims=True)
+        spot = lax.broadcasted_iota(jnp.int32, (B, LANES), 1) == lax.broadcasted_iota(
+            jnp.int32, (B, LANES), 0
+        )
+        squares[o] = jnp.sum(jnp.where(spot, each, 0.0), axis=0, keepdims=True)
+        push(6, tail_sem.at[2], squares.at[o])
+
+    for send, ref in ((2, att), (3, mix)):
+        sent(send, ref.at[pl.ds(0, T - 1)])
+    sent(1, page_stage.at[pl.ds(0, T - 1)])
+
+    @pl.when(me < q_devs)
+    def _():
+        sent(0, proj.at[0])
+
+    @pl.when(me >= q_devs)
+    def _():
+        sent(0, proj.at[pl.ds(0, T - 1)])
+
+    @pl.when(is_owner)
+    def _():
+        sent(4, arrive.at[pl.ds(0, owner_count - 1)])
+        landed(tail_sem.at[2], squares.at[pl.ds(0, owner_count - 1)])
+
+    @pl.when(jnp.logical_not(is_owner))
+    def _():
+        sent(4, arrive.at[pl.ds(0, owner_count)])
+        landed(tail_sem.at[2], squares.at[pl.ds(0, owner_count)])
+
+    @pl.when(first_owner + me // 2 != me)
+    def _():
+        landed(tail_sem.at[1], sums.at[2])
+
     sumsq = squares[0]
-    for s in range(1, T):
+    for s in range(1, owner_count):
         sumsq = sumsq + squares[s]
-    branch_ms = sumsq[:, 0:1] * (1.0 / model)
-    result = mine + normed_by(summed, branch_ms, own_gain[3:4, :])
+    spot = lax.broadcasted_iota(jnp.int32, (B, LANES), 1) == lax.broadcasted_iota(
+        jnp.int32, (B, LANES), 0
+    )
+    branch_ms = jnp.sum(
+        jnp.where(spot, jnp.broadcast_to(sumsq, (B, LANES)), 0.0), axis=-1, keepdims=True
+    ) * (1.0 / model)
+    result = mine + normed_by(sums[2], branch_ms, own_gain[3:4, :])
     out_ref[...] = result[:, :R]
-    drain(5, lambda p: squares.at[me], squares.at[me])
-    store.wait()
-
-
-def finish_kernel(out_ref, dec_ref, out_done, dec_done):
-    out_done[...] = out_ref[...]
-    dec_done[...] = dec_ref[...]
+
+    @pl.when(is_owner)
+    def _():
+        o = me - first_owner
+        sent(6, arrive_like(squares, T - 1, owner_count))
+
+        @pl.when(o * 2 == me)
+        def _():
+            sent(5, sums.at[0])
+
+        @pl.when(o * 2 + 1 == me)
+        def _():
+            sent(5, sums.at[0])
+
+        @pl.when((o * 2 != me) & (o * 2 + 1 != me))
+        def _():
+            sent(5, sums.at[pl.ds(0, 2)])
+
+
+def arrive_like(squares, count, limit):
+    return squares.at[pl.ds(0, count)]
+
+
+def finish_kernel(out_ref, dec_ref, out_hbm, dec_hbm, sem):
+    first = pltpu.make_async_copy(dec_ref, dec_hbm, sem.at[0])
+    second = pltpu.make_async_copy(out_ref, out_hbm, sem.at[1])
+    first.start()
+    second.start()
+    first.wait()
+    second.wait()
 
 
 def fits_kernel(shapes, devices):
@@ -579,20 +700,21 @@
     groups = devices // PREFILL_TP
     weight_bytes = 2 * (cols * model + rows * HEADS * HEAD_DIM + 3 * ff * model)
     return (
-        cols == HEADS // PREFILL_TP * HEAD_DIM
+        devices == 2 * PREFILL_TP
+        and cols == HEADS // PREFILL_TP * HEAD_DIM
         and (KV_HEADS * HEAD_DIM) % cols == 0
         and (HEADS * HEAD_DIM) % cols == 0
         and batch_rows % groups == 0
-        and model % LANES == 0
-        and ff % LANES == 0
+        and model % (LANES * 2) == 0
+        and ff % (6 * SUBLANES) == 0
         and rows * devices == model
+        and rows * 4 % LANES == 0
         and weight_bytes < VMEM_LIMIT * 3 // 4
         and batch_rows <= 8
     )
 
 
-def largest_tile(total, limit):
-    return max(t for t in range(LANES, limit + 1, LANES) if total % t == 0)
+SUBLANES = 16
 
 
 def fused_device(
@@ -619,25 +741,33 @@
     RP = -(-R // LANES) * LANES
     ff = down_weight.shape[1]
     k_cols = KV_HEADS * HEAD_DIM
+    planes = 4
+    plane_size = T // planes
+    owner_count = T // 2
+    depth = model // 256
+    marks = [0, depth // 3, 2 * (depth // 3), depth - 2, depth]
     dims = dict(
         T=T, B=B, R=R, RP=RP, S=S, share=share, local_heads=local_heads,
-        per_group=per_group, groups=groups,
-        ff_tile=largest_tile(ff, 384), out_tile=largest_tile(model, 512),
+        per_group=per_group, groups=groups, planes=planes, plane_size=plane_size,
+        first_owner=plane_size, owner_count=owner_count, seat_shift=R % LANES,
+        cuts=[(lo * 256, hi * 256) for lo, hi in zip(marks, marks[1:])],
+        ff_tile=ff // 6,
     )
     q_width = local_heads * share * HEAD_DIM
+    span = -(-(model // owner_count) // LANES) * LANES
     bf16, f32 = jnp.bfloat16, jnp.float32
-    smem = pl.BlockSpec(memory_space=pltpu.SMEM)
     vmem = pl.BlockSpec(memory_space=pltpu.VMEM)
     anyw = pl.BlockSpec(memory_space=pl.ANY)
     out, dec = pl.pallas_call(
         functools.partial(fused_kernel, dims),
         out_shape=(
-            jax.ShapeDtypeStruct((B, R), f32),
-            jax.ShapeDtypeStruct((2, B, page_width, k_cols), bf16),
+            pltpu.VMEM((B, R), f32),
+            pltpu.VMEM((2, B, page_width, k_cols), bf16),
         ),
-        in_specs=[smem] + [anyw] * 8,
-        out_specs=(vmem, anyw),
+        in_specs=[anyw] * 9,
+        out_specs=(vmem, vmem),
         scratch_shapes=[
+            pltpu.SMEM((B,), jnp.int32),
             pltpu.VMEM((B, model + RP), f32),
             pltpu.VMEM((norm_gains.shape[1], model + RP), f32),
             pltpu.VMEM((B, T), jnp.int32),
@@ -650,17 +780,19 @@
             pltpu.VMEM((T, per_group, q_width), bf16),
             pltpu.VMEM((B, HEADS * HEAD_DIM), bf16),
             pltpu.VMEM((T, B, RP), bf16),
-            pltpu.VMEM((B, ff), bf16),
-            pltpu.VMEM((B, model), f32),
-            pltpu.VMEM((T, B, RP), bf16),
-            pltpu.VMEM((T, B, RP), bf16),
-            pltpu.VMEM((T, B, LANES), f32),
+            pltpu.VMEM((B, model), bf16),
+            pltpu.VMEM((T, B, span), bf16),
+            pltpu.VMEM((3, B, RP), f32),
+            pltpu.VMEM((T, 1, LANES), f32),
+            pltpu.VMEM((-(-ff // (2 * LANES)) * LANES, LANES), f32),
             pltpu.VMEM((T, 2, per_group, page_width, width), bf16),
             pltpu.VMEM((2, B, page_width, k_cols), bf16),
-            pltpu.VMEM((2, B, page_width, k_cols), bf16),
+            pltpu.SemaphoreType.DMA((12,)),
+            pltpu.SemaphoreType.DMA((7,)),
             pltpu.SemaphoreType.DMA((9,)),
-            pltpu.SemaphoreType.DMA((6, T)),
-            pltpu.SemaphoreType.DMA((6, T)),
+            pltpu.SemaphoreType.DMA((4,)),
+            pltpu.SemaphoreType.DMA((4,)),
+            pltpu.SemaphoreType.DMA((4,)),
         ],
         compiler_params=pltpu.CompilerParams(
             collective_id=0, has_side_effects=True, vmem_limit_bytes=VMEM_LIMIT
@@ -679,12 +811,16 @@
     out, dec = pl.pallas_call(
         finish_kernel,
         out_shape=(
-            jax.ShapeDtypeStruct(out.shape, f32),
-            jax.ShapeDtypeStruct(dec.shape, bf16),
+            jax.ShapeDtypeStruct((B, R), f32),
+            jax.ShapeDtypeStruct((2, B, page_width, k_cols), bf16),
         ),
         in_specs=[vmem, vmem],
-        out_specs=(vmem, vmem),
-    )(out, dec)
+        out_specs=(anyw, anyw),
+        scratch_shapes=[pltpu.SemaphoreType.DMA((2,))],
+    )(
+        pltpu.with_memory_space_constraint(out, pltpu.VMEM),
+        pltpu.with_memory_space_constraint(dec, pltpu.VMEM),
+    )
     return out, dec.reshape(1, 1, 2, B, page_width, k_cols)
 
 

time: 44.5 us -> 35.4 us (0.80)
  Pallas kernels: 43.6 us -> 34.6 us
    pallas_call x2, Pallas kernels: 43.6 us -> 34.6 us  [the longest x1 33.9 us: fused_device(): pl.pallas_call(functools.partial(fused_kernel, dims), out_shape=(pltpu.VM...]
where the time goes in v1:
time: 35.4 us; the launch traced here: 35.3 us
  Pallas kernels  34.6 us (98%)
  between operations  0.64 us (2%)
    pallas_call x1, Pallas kernels, fused_device(): pl.pallas_call(functools.partial(fused_kernel, dims), out_shape=(pltpu.VM...  33.9 us
    pallas_call x1, Pallas kernels, fused_device(): pl.pallas_call(finish_kernel, out_shape=(jax.ShapeDtypeStruct((B, R), f32...  0.72 us

profile of v1, /device:TPU:0, one launch (start us, length us, event | category | flops | bytes accessed | tf_op | source)
XLA Modules:
  0.0 35.3 jit_solution(6865031256920535181)
XLA Ops:
  0.6 33.9 %shard_map.104 = (f32[4,288]{1,0:T(4,128)S(1)}, bf16[2,4,8,2048]{3,2,1,0:T(8,128)(2,1)S(1)}) custom-call(s32[4]{0:T(128)} %len_hbm.1, s32[4,16]{1,0:T(4,128)} %table_hbm.1, f32[4,4608]{1,0:T(4,128)} %hid_hbm.1, f32[4,4608]{1,0:T(4,128)} %bitcast.12, bf16[2,2,128,256]{3,2,1,0:T(8,128)(2,1)} %bitcast.11, bf16[512,4608]{1,0:T(8,128)(2,1)} %bitcast.9, ...), custom_call_target="tpu_custom_call" | custom-call | tf_op jit(solution)/shard_map/pallas_call | solution.py:761
  34.6 0.7 %shard_map.105 = (f32[4,288]{1,0:T(4,128)}, bf16[2,4,8,2048]{3,2,1,0:T(8,128)(2,1)}) custom-call(f32[4,288]{1,0:T(4,128)S(1)} %get-tuple-element.6.out_ref, bf16[2,4,8,2048]{3,2,1,0:T(8,128)(2,1)S(1)} %get-tuple-element.7.dec_ref), custom_call_target="tpu_custom_call" | custom-call | tf_op jit(solution)/shard_map/pallas_call | solution.py:811

commit v2 on v1

--- a/solution.py
+++ b/solution.py
@@ -247,7 +247,9 @@
     arrive,
     sums,
     squares,
-    turned_act,
+    stack,
+    mixed_ref,
+    blend,
     page_stage,
     dec,
     load_sem,
@@ -361,8 +363,6 @@
             peer = lax.rem(me + step, T)
             remote(page_stage.at[peer], dec_part(dec, me), 1, tail_sem.at[3], peer).start()
 
-    share_of = -(-(T - 1) // 4)
-
     def push(send, recv, src):
         for step in range(1, T):
             peer = lax.rem(me + step, T)
@@ -434,7 +434,7 @@
         for c in range(2):
             moved = jnp.dot(pick, flat[c, e], preferred_element_type=jnp.float32)
             page_stage[:, c, e] = moved.reshape(T, page_width, width).astype(jnp.bfloat16)
-    push_pages(1, 1 + share_of)
+    push_pages(1, dims["page_cut"])
     q_from, k_from, v_from = owners(me)
     take_proj(q_from)
     take_proj(k_from)
@@ -479,7 +479,6 @@
             at = (a * share + m) * HEAD_DIM
             att[me, :, at : at + HEAD_DIM] = jnp.concatenate(picked[m], axis=0).astype(jnp.bfloat16)
     push(2, att_sem.at[my_plane], att.at[me])
-    push_pages(1 + share_of, 1 + 2 * share_of)
 
     first_lane = pl.multiple_of(me * R // LANES * LANES, LANES)
     window = RP + LANES
@@ -515,46 +514,80 @@
     shift = dims["seat_shift"]
     mix[me] = pltpu.roll(mixed, my_seat * shift, 1).astype(jnp.bfloat16)
     push(3, mix_sem.at[my_plane], mix.at[me])
-    push_pages(1 + 2 * share_of, 1 + 3 * share_of)
-    for step in range(planes):
-        take_plane(mix_sem, mix, jnp.int32(step))
-
-    gathered = [None] * chunks
-    for s in range(T):
-        block = mix[s].astype(jnp.float32)
-        for i in range(RP // LANES):
-            at = s * R // LANES + i
-            tile = block[:, i * LANES : (i + 1) * LANES]
-            if at < chunks:
-                gathered[at] = tile if gathered[at] is None else gathered[at] + tile
-    mixed_all = jnp.concatenate(gathered, axis=1)
-    mixed_ms = meansq_of(mixed_all)
-    stream = hid[:, :model] + normed_by(mixed_all, mixed_ms, gain[1:2, :model])
-    ffn_in = normed_by(stream, meansq_of(stream), gain[2:3, :model]).astype(jnp.bfloat16)
-    mine = own_hid + normed_by(mixed, mixed_ms, own_gain[1:2, :])
-
-    push_pages(1 + 3 * share_of, T)
+    blend[:B, :] = hid[:, :model] * (1.0 + gain[2:3, :model])
     wgu_load.wait()
     side = ff // 2
     tile = dims["ff_tile"]
-    probe = pad_rows(ffn_in, SUBLANES)
-    fronts = []
     at_lane = tile // LANES * LANES
-    for at in range(0, side, tile):
-        flatwise = []
-        upright = []
-        for c in range(2):
-            pushed = jnp.concatenate([wgu[c, at : at + tile, :], probe], axis=0)
-            passed = jnp.concatenate([probe, wgu[c, side + at : side + at + tile, :]], axis=0)
+    blocks = [(s, c) for s in range(side // tile) for c in range(2)]
+    half_cols = model // halves
+    half_seats = T // halves
+    front, upright = {}, {}
+    for turn_of in range(halves):
+        which = (my_plane // (planes // halves) + turn_of) % halves
+        for p in range(planes // halves):
+            plane = which * (planes // halves) + p
+            if turn_of:
+                landed(mix_sem.at[plane], mix.at[pl.ds(plane * plane_size, plane_size)])
+            else:
+                take_plane(mix_sem, mix, plane)
+        if turn_of == 0:
+            push_pages(dims["page_cut"], T)
+            send_projections(False)
+        tiles = [None] * (half_cols // LANES)
+        for s in range(half_seats):
+            block = mix[which * half_seats + s].astype(jnp.float32)
+            for i in range(RP // LANES):
+                at = s * R // LANES + i
+                piece = block[:, i * LANES : (i + 1) * LANES]
+                if at < len(tiles):
+                    tiles[at] = piece if tiles[at] is None else tiles[at] + piece
+        got = jnp.concatenate(tiles, axis=1)
+        span_at = pl.ds(pl.multiple_of(which * half_cols, LANES), half_cols)
+        mixed_ref[:, span_at] = got
+        blend[B:, span_at] = got * ((1.0 + gain[1:2, span_at]) * (1.0 + gain[2:3, span_at]))
+        exact = blend[:, span_at]
+        high = exact.astype(jnp.bfloat16).astype(jnp.float32)
+        probe = jnp.concatenate([high, exact - high], axis=0).astype(jnp.bfloat16)
+        if turn_of == halves - 1:
+            mixed_all = mixed_ref[...]
+            mixed_ms = meansq_of(mixed_all)
+            stream = hid[:, :model] + normed_by(mixed_all, mixed_ms, gain[1:2, :model])
+            outer = lax.rsqrt(meansq_of(stream) + EPSILON)
+            inner = lax.rsqrt(mixed_ms + EPSILON)
+            mine = own_hid + normed_by(mixed, mixed_ms, own_gain[1:2, :])
+        for s, c in blocks:
+            at = s * tile
+            pushed = jnp.concatenate([wgu[c, at : at + tile, span_at], probe], axis=0)
+            passed = jnp.concatenate(
+                [probe, wgu[c, side + at : side + at + tile, span_at]], axis=0
+            )
             both = dot_t(passed, pushed)
-            flatwise.append(both[:B, :tile])
-            upright.append(both[SUBLANES:, at_lane:])
-        fronts.append(jax.nn.gelu(flatwise[0], approximate=True) * flatwise[1])
-        turned_act[at : at + tile, : upright[0].shape[1]] = (
-            jax.nn.gelu(upright[0], approximate=True) * upright[1]
-        )
-    back = turned_act[...].T[tile - at_lane : tile - at_lane + B, :side]
-    active = jnp.concatenate(fronts + [back], axis=1).astype(jnp.bfloat16)
+            part = both[: 2 * B, :tile] + both[2 * B : 4 * B, :tile]
+            front[s, c] = part if turn_of == 0 else front[s, c] + part
+            rest = both[4 * B :, at_lane:]
+            wide = rest.shape[1]
+            if turn_of < halves - 1:
+                stack[s, c, :, :wide] = rest
+            else:
+                rest = jnp.concatenate(
+                    [rest + stack[s, c, :, :wide], jnp.zeros((tile, LANES - wide), jnp.float32)],
+                    axis=1,
+                )
+                turned = rest.T
+                first = tile - at_lane
+                upright[s, c] = turned[first : first + 2 * B] + turned[first + 2 * B : first + 4 * B]
+
+    def settle(parts):
+        return outer * (parts[:B] + inner * parts[B:])
+
+    steps = range(side // tile)
+    active = []
+    for table_of in (front, upright):
+        for s in steps:
+            gate, up = settle(table_of[s, 0]), settle(table_of[s, 1])
+            active.append(jax.nn.gelu(gate, approximate=True) * up)
+    active = jnp.concatenate(active, axis=1).astype(jnp.bfloat16)
     wd_load.wait()
     branch[...] = jnp.dot(active, wd[...], preferred_element_type=jnp.float32).astype(jnp.bfloat16)
 
@@ -568,24 +601,6 @@
         def _():
             piece = branch.at[:, pl.ds(o * owned // LANES * LANES, span)]
             remote(piece, arrive.at[me], 4, tail_sem.at[0], jnp.int32(peer)).start()
-
-    send_projections(False)
-    dec_part(dec, me)[...] = page_stage[me]
-    landed(tail_sem.at[3], page_stage.at[pl.ds(0, T - 1)])
-    for owner in range(q_devs, q_devs + 2 * k_devs):
-        @pl.when((owner != k_from) & (owner != v_from))
-        def _():
-            take_proj(jnp.int32(owner))
-
-    token = lax.broadcasted_iota(jnp.int32, (page_width, cols), 0) + me * page_width
-    for c in range(2):
-        for i in range(k_devs):
-            fresh = proj[q_devs + c * k_devs + i].astype(jnp.float32)
-            for r in range(B):
-                old = dec[c, r, :, i * cols : (i + 1) * cols].astype(jnp.float32)
-                row = jnp.broadcast_to(fresh[r : r + 1, :], old.shape)
-                new = jnp.where(token == len_ref[r], row, old)
-                dec_done[c, r, :, i * cols : (i + 1) * cols] = new.astype(jnp.bfloat16)
 
     @pl.when(is_owner)
     def _():
@@ -625,6 +640,23 @@
         squares[o] = jnp.sum(jnp.where(spot, each, 0.0), axis=0, keepdims=True)
         push(6, tail_sem.at[2], squares.at[o])
 
+    dec_part(dec, me)[...] = page_stage[me]
+    landed(tail_sem.at[3], page_stage.at[pl.ds(0, T - 1)])
+    for owner in range(q_devs, q_devs + 2 * k_devs):
+        @pl.when((owner != k_from) & (owner != v_from))
+        def _():
+            take_proj(jnp.int32(owner))
+
+    token = lax.broadcasted_iota(jnp.int32, (page_width, cols), 0) + me * page_width
+    for c in range(2):
+        for i in range(k_devs):
+            fresh = proj[q_devs + c * k_devs + i].astype(jnp.float32)
+            for r in range(B):
+                old = dec[c, r, :, i * cols : (i + 1) * cols].astype(jnp.float32)
+                row = jnp.broadcast_to(fresh[r : r + 1, :], old.shape)
+                new = jnp.where(token == len_ref[r], row, old)
+                dec_done[c, r, :, i * cols : (i + 1) * cols] = new.astype(jnp.bfloat16)
+
     for send, ref in ((2, att), (3, mix)):
         sent(send, ref.at[pl.ds(0, T - 1)])
     sent(1, page_stage.at[pl.ds(0, T - 1)])
@@ -710,7 +742,7 @@
         and rows * devices == model
         and rows * 4 % LANES == 0
         and weight_bytes < VMEM_LIMIT * 3 // 4
-        and batch_rows <= 8
+        and batch_rows == 4
     )
 
 
@@ -745,13 +777,13 @@
     plane_size = T // planes
     owner_count = T // 2
     depth = model // 256
-    marks = [0, depth // 3, 2 * (depth // 3), depth - 2, depth]
+    marks = list(range(0, depth, 2)) + [depth]
     dims = dict(
         T=T, B=B, R=R, RP=RP, S=S, share=share, local_heads=local_heads,
         per_group=per_group, groups=groups, planes=planes, plane_size=plane_size,
         first_owner=plane_size, owner_count=owner_count, seat_shift=R % LANES,
         cuts=[(lo * 256, hi * 256) for lo, hi in zip(marks, marks[1:])],
-        ff_tile=ff // 6,
+        ff_tile=ff // 6, page_cut=T // 2,
     )
     q_width = local_heads * share * HEAD_DIM
     span = -(-(model // owner_count) // LANES) * LANES
@@ -784,10 +816,12 @@
             pltpu.VMEM((T, B, span), bf16),
             pltpu.VMEM((3, B, RP), f32),
             pltpu.VMEM((T, 1, LANES), f32),
-            pltpu.VMEM((-(-ff // (2 * LANES)) * LANES, LANES), f32),
+            pltpu.VMEM((3, 2, ff // 6, LANES), f32),
+            pltpu.VMEM((B, model), f32),
+            pltpu.VMEM((2 * B, model), f32),
             pltpu.VMEM((T, 2, per_group, page_width, width), bf16),
             pltpu.VMEM((2, B, page_width, k_cols), bf16),
-            pltpu.SemaphoreType.DMA((12,)),
+            pltpu.SemaphoreType.DMA((8 + len(dims["cuts"]),)),
             pltpu.SemaphoreType.DMA((7,)),
             pltpu.SemaphoreType.DMA((9,)),
             pltpu.SemaphoreType.DMA((4,)),

time: 35.4 us -> 32.7 us (0.924)
  Pallas kernels: 34.6 us -> 31.9 us
    pallas_call x1, Pallas kernels: 33.9 us -> 31.2 us  [fused_device(): pl.pallas_call(functools.partial(fused_kernel, dims), out_shape=(pltpu.VM...]
where the time goes in v2:
time: 32.7 us; the launch traced here: 32.5 us
  Pallas kernels  31.9 us (98%)
  between operations  0.64 us (2%)
    pallas_call x1, Pallas kernels, fused_device(): pl.pallas_call(functools.partial(fused_kernel, dims), out_shape=(pltpu.VM...  31.2 us
    pallas_call x1, Pallas kernels, fused_device(): pl.pallas_call(finish_kernel, out_shape=(jax.ShapeDtypeStruct((B, R), f32...  0.72 us

profile of v2, /device:TPU:0, one launch (start us, length us, event | category | flops | bytes accessed | tf_op | source)
XLA Modules:
  0.0 32.5 jit_solution(10391029101649215534)
XLA Ops:
  0.6 31.2 %shard_map.104 = (f32[4,288]{1,0:T(4,128)S(1)}, bf16[2,4,8,2048]{3,2,1,0:T(8,128)(2,1)S(1)}) custom-call(s32[4]{0:T(128)} %len_hbm.1, s32[4,16]{1,0:T(4,128)} %table_hbm.1, f32[4,4608]{1,0:T(4,128)} %hid_hbm.1, f32[4,4608]{1,0:T(4,128)} %bitcast.12, bf16[2,2,128,256]{3,2,1,0:T(8,128)(2,1)} %bitcast.11, bf16[512,4608]{1,0:T(8,128)(2,1)} %bitcast.9, ...), custom_call_target="tpu_custom_call" | custom-call | tf_op jit(solution)/shard_map/pallas_call | solution.py:793
  31.8 0.7 %shard_map.105 = (f32[4,288]{1,0:T(4,128)}, bf16[2,4,8,2048]{3,2,1,0:T(8,128)(2,1)}) custom-call(f32[4,288]{1,0:T(4,128)S(1)} %get-tuple-element.6.out_ref, bf16[2,4,8,2048]{3,2,1,0:T(8,128)(2,1)S(1)} %get-tuple-element.7.dec_ref), custom_call_target="tpu_custom_call" | custom-call | tf_op jit(solution)/shard_map/pallas_call | solution.py:845

commit v3 on v2

--- a/solution.py
+++ b/solution.py
@@ -298,17 +298,14 @@
     wo_load = load(5, wo_hbm, wo)
     wgu_load = load(6, wgu_hbm, wgu)
     wd_load = load(7, wd_hbm, wd)
-    for piece in small + wq_loads + [flat_load]:
+    for piece in small + wq_loads + [flat_load, wo_load, wgu_load, wd_load]:
         piece.start()
 
     barrier = pltpu.get_barrier_semaphore()
 
-    def greet(step, carry):
+    for step in range(1, T):
         peer = lax.rem(me + step, T)
         pl.semaphore_signal(barrier, inc=1, device_id={"tp": peer}, device_id_type=MESH)
-        return carry
-
-    lax.fori_loop(1, T, greet, 0)
 
     def dec_part(ref, index):
         group, slot = index // PREFILL_TP, index % PREFILL_TP
@@ -342,14 +339,31 @@
     def send_proj(peer):
         remote(proj.at[me], proj.at[me], 0, proj_from(me), peer).start()
 
-    def send_projections(urgent):
+    def send_urgent():
+        @pl.when(me < q_devs)
+        def _():
+            send_proj(me + PREFILL_TP)
+
+        @pl.when(me >= q_devs)
+        def _():
+            first = (me - q_devs) % k_devs * (PREFILL_TP // k_devs)
+            for g in range(groups):
+                for i in range(PREFILL_TP // k_devs):
+                    peer = g * PREFILL_TP + first + i
+                    if g == 0:
+                        send_proj(peer)
+                        continue
+
+                    @pl.when(peer != me)
+                    def _():
+                        send_proj(peer)
+
+    def send_others():
         for step in range(1, T):
             peer = lax.rem(me + step, T)
             q_owner, k_owner, v_owner = owners(peer)
-            hurry = (q_owner == me) | (k_owner == me) | (v_owner == me)
-            wanted = hurry if urgent else jnp.logical_not(hurry) & (me >= q_devs)
-
-            @pl.when(wanted)
+
+            @pl.when((k_owner != me) & (v_owner != me) & (me >= q_devs))
             def _():
                 send_proj(peer)
 
@@ -363,10 +377,22 @@
             peer = lax.rem(me + step, T)
             remote(page_stage.at[peer], dec_part(dec, me), 1, tail_sem.at[3], peer).start()
 
-    def push(send, recv, src):
-        for step in range(1, T):
-            peer = lax.rem(me + step, T)
-            remote(src, src, send, recv, peer).start()
+    def push(send, recv, src, near_first=False):
+        upper = my_plane // (planes // 2)
+        for turn_of in range(planes):
+            if near_first:
+                plane = jnp.where(upper == 0, turn_of, planes - 1 - turn_of)
+            else:
+                plane = jnp.where(upper == 0, planes - 1 - turn_of, turn_of)
+            for seat in range(plane_size):
+                peer = plane * plane_size + lax.rem(my_seat + seat, plane_size)
+                if seat:
+                    remote(src, src, send, recv, peer).start()
+                    continue
+
+                @pl.when(plane != my_plane)
+                def _():
+                    remote(src, src, send, recv, peer).start()
 
     def take_plane(sems, ref, plane):
         first = plane * plane_size
@@ -414,9 +440,6 @@
     part = jnp.zeros((B, cols), jnp.float32)
     for (lo, hi), piece in zip(cuts, wq_loads):
         piece.wait()
-        if hi == model:
-            for late in (wo_load, wgu_load, wd_load):
-                late.start()
         part = part + dot_t(normed[:, lo:hi], wq[:, lo:hi])
     part = part.astype(jnp.bfloat16).astype(jnp.float32)
     for head in range(heads_here):
@@ -425,7 +448,7 @@
         turned = u * cosine + swapped * sine
         proj[me, :, head * HEAD_DIM : (head + 1) * HEAD_DIM] = turned.astype(jnp.bfloat16)
     pl.semaphore_wait(barrier, T - 1)
-    send_projections(True)
+    send_urgent()
 
     flat_load.wait()
     wanted = lax.broadcasted_iota(jnp.int32, (slots, slots), 0).astype(jnp.float32)
@@ -479,6 +502,7 @@
             at = (a * share + m) * HEAD_DIM
             att[me, :, at : at + HEAD_DIM] = jnp.concatenate(picked[m], axis=0).astype(jnp.bfloat16)
     push(2, att_sem.at[my_plane], att.at[me])
+    send_others()
 
     first_lane = pl.multiple_of(me * R // LANES * LANES, LANES)
     window = RP + LANES
@@ -490,30 +514,29 @@
     halves = T // PREFILL_TP
     slots_half = PREFILL_TP // halves
     half_width = slots_half * q_width
-    mixed = jnp.zeros((B, R), jnp.float32)
-    for turn_of in range(halves):
-        which = (my_plane // (planes // halves) + turn_of) % halves
-        for g in range(groups):
-            take_plane(att_sem, att, g * halves + which)
-        blocks = [
-            jnp.concatenate(
-                [
-                    att[g * PREFILL_TP + which * slots_half + s].astype(jnp.float32)
-                    for g in range(groups)
-                ],
-                axis=0,
-            ).astype(jnp.bfloat16)
-            for s in range(slots_half)
-        ]
-        lane_at = pl.multiple_of(which * half_width, half_width)
-        mixed = mixed + dot_t(
-            jnp.concatenate(blocks, axis=1), wo[:, pl.ds(lane_at, half_width)]
+    for p in range(planes):
+        take_plane(att_sem, att, jnp.int32(p))
+    pieces = [
+        jnp.concatenate(
+            [att[g * PREFILL_TP + s].astype(jnp.float32) for g in range(groups)], axis=0
         )
+        for s in range(PREFILL_TP)
+    ]
+    probe = pad_rows(jnp.concatenate(pieces, axis=1).astype(jnp.bfloat16), SUBLANES)
+    pair = R // 2
+    pair_lane = pair // LANES * LANES
+    both = dot_t(
+        jnp.concatenate([probe, wo[pair:, :]], axis=0),
+        jnp.concatenate([wo[:pair, :], probe], axis=0),
+    )
+    rest = both[SUBLANES:, pair_lane:]
+    rest = jnp.concatenate([rest, jnp.zeros((pair, LANES - rest.shape[1]), jnp.float32)], axis=1).T
+    mixed = jnp.concatenate([both[:B, :pair], rest[pair - pair_lane : pair - pair_lane + B]], axis=1)
     mixed = mixed.astype(jnp.bfloat16).astype(jnp.float32)
     mixed = jnp.concatenate([mixed, jnp.zeros((B, RP - R), jnp.float32)], axis=1)
     shift = dims["seat_shift"]
     mix[me] = pltpu.roll(mixed, my_seat * shift, 1).astype(jnp.bfloat16)
-    push(3, mix_sem.at[my_plane], mix.at[me])
+    push(3, mix_sem.at[my_plane], mix.at[me], True)
     blend[:B, :] = hid[:, :model] * (1.0 + gain[2:3, :model])
     wgu_load.wait()
     side = ff // 2
@@ -533,7 +556,6 @@
                 take_plane(mix_sem, mix, plane)
         if turn_of == 0:
             push_pages(dims["page_cut"], T)
-            send_projections(False)
         tiles = [None] * (half_cols // LANES)
         for s in range(half_seats):
             block = mix[which * half_seats + s].astype(jnp.float32)
@@ -589,18 +611,25 @@
             active.append(jax.nn.gelu(gate, approximate=True) * up)
     active = jnp.concatenate(active, axis=1).astype(jnp.bfloat16)
     wd_load.wait()
-    branch[...] = jnp.dot(active, wd[...], preferred_element_type=jnp.float32).astype(jnp.bfloat16)
-
     owned = model // owner_count
     span = arrive.shape[2]
     is_owner = (me >= first_owner) & (me < first_owner + owner_count)
-    for o in range(owner_count):
-        peer = first_owner + o
-
-        @pl.when(me != peer)
-        def _():
-            piece = branch.at[:, pl.ds(o * owned // LANES * LANES, span)]
-            remote(piece, arrive.at[me], 4, tail_sem.at[0], jnp.int32(peer)).start()
+    side_owners = owner_count // halves
+    for turn_of in range(halves):
+        which = (halves - 1 - my_plane // (planes // halves) + turn_of) % halves
+        half_at = pl.multiple_of(which * half_cols, LANES)
+        wide = -(-half_cols // (4 * LANES)) * 4 * LANES
+        done_cols = wide if turn_of == 0 else model - wide
+        done_at = pl.multiple_of(which * (model - done_cols), LANES)
+        part = jnp.dot(active, wd[:, pl.ds(done_at, done_cols)], preferred_element_type=jnp.float32)
+        branch[:, pl.ds(done_at, done_cols)] = part.astype(jnp.bfloat16)
+        for i in range(side_owners):
+            peer = first_owner + which * side_owners + i
+
+            @pl.when(me != peer)
+            def _():
+                begin = pl.multiple_of(half_at + i * owned // LANES * LANES, LANES)
+                remote(branch.at[:, pl.ds(begin, span)], arrive.at[me], 4, tail_sem.at[0], peer).start()
 
     @pl.when(is_owner)
     def _():
@@ -741,6 +770,7 @@
         and ff % (6 * SUBLANES) == 0
         and rows * devices == model
         and rows * 4 % LANES == 0
+        and rows % (2 * SUBLANES) == 0
         and weight_bytes < VMEM_LIMIT * 3 // 4
         and batch_rows == 4
     )

time: 32.7 us -> 32.2 us (0.985)
  Pallas kernels: 31.9 us -> 31.4 us
    pallas_call x1, Pallas kernels: 31.2 us -> 30.7 us  [fused_device(): pl.pallas_call(functools.partial(fused_kernel, dims), out_shape=(pltpu.VM...]
where the time goes in v3:
time: 32.2 us; the launch traced here: 32.1 us
  Pallas kernels  31.4 us (98%)
  between operations  0.64 us (2%)
    pallas_call x1, Pallas kernels, fused_device(): pl.pallas_call(functools.partial(fused_kernel, dims), out_shape=(pltpu.VM...  30.7 us
    pallas_call x1, Pallas kernels, fused_device(): pl.pallas_call(finish_kernel, out_shape=(jax.ShapeDtypeStruct((B, R), f32...  0.72 us

profile of v3, /device:TPU:0, one launch (start us, length us, event | category | flops | bytes accessed | tf_op | source)
XLA Modules:
  0.0 32.1 jit_solution(3207501286184888902)
XLA Ops:
  0.6 30.7 %shard_map.104 = (f32[4,288]{1,0:T(4,128)S(1)}, bf16[2,4,8,2048]{3,2,1,0:T(8,128)(2,1)S(1)}) custom-call(s32[4]{0:T(128)} %len_hbm.1, s32[4,16]{1,0:T(4,128)} %table_hbm.1, f32[4,4608]{1,0:T(4,128)} %hid_hbm.1, f32[4,4608]{1,0:T(4,128)} %bitcast.12, bf16[2,2,128,256]{3,2,1,0:T(8,128)(2,1)} %bitcast.11, bf16[512,4608]{1,0:T(8,128)(2,1)} %bitcast.9, ...), custom_call_target="tpu_custom_call" | custom-call | tf_op jit(solution)/shard_map/pallas_call | solution.py:823
  31.4 0.7 %shard_map.105 = (f32[4,288]{1,0:T(4,128)}, bf16[2,4,8,2048]{3,2,1,0:T(8,128)(2,1)}) custom-call(f32[4,288]{1,0:T(4,128)S(1)} %get-tuple-element.6.out_ref, bf16[2,4,8,2048]{3,2,1,0:T(8,128)(2,1)S(1)} %get-tuple-element.7.dec_ref), custom_call_target="tpu_custom_call" | custom-call | tf_op jit(solution)/shard_map/pallas_call | solution.py:875

commit v4 on v3

--- a/solution.py
+++ b/solution.py
@@ -525,13 +525,27 @@
     probe = pad_rows(jnp.concatenate(pieces, axis=1).astype(jnp.bfloat16), SUBLANES)
     pair = R // 2
     pair_lane = pair // LANES * LANES
-    both = dot_t(
-        jnp.concatenate([probe, wo[pair:, :]], axis=0),
-        jnp.concatenate([wo[:pair, :], probe], axis=0),
-    )
-    rest = both[SUBLANES:, pair_lane:]
-    rest = jnp.concatenate([rest, jnp.zeros((pair, LANES - rest.shape[1]), jnp.float32)], axis=1).T
-    mixed = jnp.concatenate([both[:B, :pair], rest[pair - pair_lane : pair - pair_lane + B]], axis=1)
+    cut = probe.shape[1] // 2
+    sides = [
+        dot_t(
+            jnp.concatenate([probe[:, k : k + cut], wo[pair:, k : k + cut]], axis=0),
+            jnp.concatenate([wo[:pair, k : k + cut], probe[:, k : k + cut]], axis=0),
+        )
+        for k in (0, cut)
+    ]
+    flatwise = jnp.concatenate([side[:B, :pair] for side in sides], axis=0)
+    flatwise = flatwise[:B] + flatwise[B:]
+    upward = [
+        jnp.concatenate(
+            [
+                side[SUBLANES:, pair_lane:],
+                jnp.zeros((pair, LANES - (SUBLANES + pair - pair_lane)), jnp.float32),
+            ],
+            axis=1,
+        ).T[pair - pair_lane : pair - pair_lane + B]
+        for side in sides
+    ]
+    mixed = jnp.concatenate([flatwise, upward[0] + upward[1]], axis=1)
     mixed = mixed.astype(jnp.bfloat16).astype(jnp.float32)
     mixed = jnp.concatenate([mixed, jnp.zeros((B, RP - R), jnp.float32)], axis=1)
     shift = dims["seat_shift"]

time: 32.2 us -> 31.3 us (0.972)
  Pallas kernels: 31.4 us -> 30.5 us
    pallas_call x1, Pallas kernels: 30.7 us -> 29.8 us  [fused_device(): pl.pallas_call(functools.partial(fused_kernel, dims), out_shape=(pltpu.VM...]
where the time goes in v4:
time: 31.3 us; the launch traced here: 31.1 us
  Pallas kernels  30.5 us (97%)
  between operations  0.64 us (2%)
    pallas_call x1, Pallas kernels, fused_device(): pl.pallas_call(functools.partial(fused_kernel, dims), out_shape=(pltpu.VM...  29.8 us
    pallas_call x1, Pallas kernels, fused_device(): pl.pallas_call(finish_kernel, out_shape=(jax.ShapeDtypeStruct((B, R), f32...  0.72 us

profile of v4, /device:TPU:0, one launch (start us, length us, event | category | flops | bytes accessed | tf_op | source)
XLA Modules:
  0.0 31.1 jit_solution(2525363008231317762)
XLA Ops:
  0.6 29.8 %shard_map.104 = (f32[4,288]{1,0:T(4,128)S(1)}, bf16[2,4,8,2048]{3,2,1,0:T(8,128)(2,1)S(1)}) custom-call(s32[4]{0:T(128)} %len_hbm.1, s32[4,16]{1,0:T(4,128)} %table_hbm.1, f32[4,4608]{1,0:T(4,128)} %hid_hbm.1, f32[4,4608]{1,0:T(4,128)} %bitcast.12, bf16[2,2,128,256]{3,2,1,0:T(8,128)(2,1)} %bitcast.11, bf16[512,4608]{1,0:T(8,128)(2,1)} %bitcast.9, ...), custom_call_target="tpu_custom_call" | custom-call | tf_op jit(solution)/shard_map/pallas_call | solution.py:837
  30.4 0.7 %shard_map.105 = (f32[4,288]{1,0:T(4,128)}, bf16[2,4,8,2048]{3,2,1,0:T(8,128)(2,1)}) custom-call(f32[4,288]{1,0:T(4,128)S(1)} %get-tuple-element.6.out_ref, bf16[2,4,8,2048]{3,2,1,0:T(8,128)(2,1)S(1)} %get-tuple-element.7.dec_ref), custom_call_target="tpu_custom_call" | custom-call | tf_op jit(solution)/shard_map/pallas_call | solution.py:889

commit v5 on v4

--- a/solution.py
+++ b/solution.py
@@ -394,17 +394,6 @@
                 def _():
                     remote(src, src, send, recv, peer).start()
 
-    def take_plane(sems, ref, plane):
-        first = plane * plane_size
-
-        @pl.when(plane == my_plane)
-        def _():
-            landed(sems.at[plane], ref.at[pl.ds(first, plane_size - 1)])
-
-        @pl.when(plane != my_plane)
-        def _():
-            landed(sems.at[plane], ref.at[pl.ds(first, plane_size)])
-
     small[2].wait()
     length = column_of(len_ref, B)
     lane = lax.broadcasted_iota(jnp.int32, (B, HEAD_DIM), 1)
@@ -501,7 +490,7 @@
         for m in range(share):
             at = (a * share + m) * HEAD_DIM
             att[me, :, at : at + HEAD_DIM] = jnp.concatenate(picked[m], axis=0).astype(jnp.bfloat16)
-    push(2, att_sem.at[my_plane], att.at[me])
+    push(2, att_sem.at[0], att.at[me])
     send_others()
 
     first_lane = pl.multiple_of(me * R // LANES * LANES, LANES)
@@ -514,8 +503,7 @@
     halves = T // PREFILL_TP
     slots_half = PREFILL_TP // halves
     half_width = slots_half * q_width
-    for p in range(planes):
-        take_plane(att_sem, att, jnp.int32(p))
+    landed(att_sem.at[0], att.at[pl.ds(0, T - 1)])
     pieces = [
         jnp.concatenate(
             [att[g * PREFILL_TP + s].astype(jnp.float32) for g in range(groups)], axis=0
@@ -550,7 +538,7 @@
     mixed = jnp.concatenate([mixed, jnp.zeros((B, RP - R), jnp.float32)], axis=1)
     shift = dims["seat_shift"]
     mix[me] = pltpu.roll(mixed, my_seat * shift, 1).astype(jnp.bfloat16)
-    push(3, mix_sem.at[my_plane], mix.at[me], True)
+    push(3, mix_sem.at[my_group], mix.at[me], True)
     blend[:B, :] = hid[:, :model] * (1.0 + gain[2:3, :model])
     wgu_load.wait()
     side = ff // 2
@@ -562,12 +550,8 @@
     front, upright = {}, {}
     for turn_of in range(halves):
         which = (my_plane // (planes // halves) + turn_of) % halves
-        for p in range(planes // halves):
-            plane = which * (planes // halves) + p
-            if turn_of:
-                landed(mix_sem.at[plane], mix.at[pl.ds(plane * plane_size, plane_size)])
-            else:
-                take_plane(mix_sem, mix, plane)
+        seats = half_seats - 1 if turn_of == 0 else half_seats
+        landed(mix_sem.at[which], mix.at[pl.ds(which * half_seats, seats)])
         if turn_of == 0:
             push_pages(dims["page_cut"], T)
         tiles = [None] * (half_cols // LANES)
@@ -606,13 +590,11 @@
             if turn_of < halves - 1:
                 stack[s, c, :, :wide] = rest
             else:
-                rest = jnp.concatenate(
-                    [rest + stack[s, c, :, :wide], jnp.zeros((tile, LANES - wide), jnp.float32)],
-                    axis=1,
-                )
-                turned = rest.T
+                rest = jnp.concatenate([rest, jnp.zeros((tile, LANES - wide), jnp.float32)], axis=1)
                 first = tile - at_lane
-                upright[s, c] = turned[first : first + 2 * B] + turned[first + 2 * B : first + 4 * B]
+                turned = [(piece.T)[first : first + 4 * B] for piece in (rest, stack[s, c])]
+                turned = turned[0] + turned[1]
+                upright[s, c] = turned[: 2 * B] + turned[2 * B :]
 
     def settle(parts):
         return outer * (parts[:B] + inner * parts[B:])
@@ -659,6 +641,12 @@
         lane_of = lax.broadcasted_iota(jnp.int32, (B, span), 1)
         inside = (lane_of >= offset) & (lane_of < offset + owned)
         kept = jnp.where(inside, total, 0.0)
+        each = jnp.sum(kept * kept, axis=-1, keepdims=True)
+        spot = lax.broadcasted_iota(jnp.int32, (B, LANES), 1) == lax.broadcasted_iota(
+            jnp.int32, (B, LANES), 0
+        )
+        squares[o] = jnp.sum(jnp.where(spot, each, 0.0), axis=0, keepdims=True)
+        push(6, tail_sem.at[2], squares.at[o])
         ready = []
         for i in range(2):
             begin = i * R // LANES * LANES
@@ -675,13 +663,6 @@
             @pl.when(peer == me)
             def _():
                 sums[2] = ready[i]
-
-        each = jnp.sum(kept * kept, axis=-1, keepdims=True)
-        spot = lax.broadcasted_iota(jnp.int32, (B, LANES), 1) == lax.broadcasted_iota(
-            jnp.int32, (B, LANES), 0
-        )
-        squares[o] = jnp.sum(jnp.where(spot, each, 0.0), axis=0, keepdims=True)
-        push(6, tail_sem.at[2], squares.at[o])
 
     dec_part(dec, me)[...] = page_stage[me]
     landed(tail_sem.at[3], page_stage.at[pl.ds(0, T - 1)])
@@ -827,7 +808,7 @@
         per_group=per_group, groups=groups, planes=planes, plane_size=plane_size,
         first_owner=plane_size, owner_count=owner_count, seat_shift=R % LANES,
         cuts=[(lo * 256, hi * 256) for lo, hi in zip(marks, marks[1:])],
-        ff_tile=ff // 6, page_cut=T // 2,
+        ff_tile=ff // 6, page_cut=6,
     )
     q_width = local_heads * share * HEAD_DIM
     span = -(-(model // owner_count) // LANES) * LANES
@@ -868,8 +849,8 @@
             pltpu.SemaphoreType.DMA((8 + len(dims["cuts"]),)),
             pltpu.SemaphoreType.DMA((7,)),
             pltpu.SemaphoreType.DMA((9,)),
-            pltpu.SemaphoreType.DMA((4,)),
-            pltpu.SemaphoreType.DMA((4,)),
+            pltpu.SemaphoreType.DMA((1,)),
+            pltpu.SemaphoreType.DMA((2,)),
             pltpu.SemaphoreType.DMA((4,)),
         ],
         compiler_params=pltpu.CompilerParams(

time: 31.3 us -> 31.1 us (level)
  no operation moved by 1% of the time
where the time goes in v5:
time: 31.1 us; the launch traced here: 31 us
  Pallas kernels  30.3 us (97%)
  between operations  0.64 us (2%)
    pallas_call x1, Pallas kernels, fused_device(): pl.pallas_call(functools.partial(fused_kernel, dims), out_shape=(pltpu.VM...  29.6 us
    pallas_call x1, Pallas kernels, fused_device(): pl.pallas_call(finish_kernel, out_shape=(jax.ShapeDtypeStruct((B, R), f32...  0.72 us

profile of v5, /device:TPU:0, one launch (start us, length us, event | category | flops | bytes accessed | tf_op | source)
XLA Modules:
  0.0 31.0 jit_solution(2600769073383393012)
XLA Ops:
  0.6 29.6 %shard_map.104 = (f32[4,288]{1,0:T(4,128)S(1)}, bf16[2,4,8,2048]{3,2,1,0:T(8,128)(2,1)S(1)}) custom-call(s32[4]{0:T(128)} %len_hbm.1, s32[4,16]{1,0:T(4,128)} %table_hbm.1, f32[4,4608]{1,0:T(4,128)} %hid_hbm.1, f32[4,4608]{1,0:T(4,128)} %bitcast.12, bf16[2,2,128,256]{3,2,1,0:T(8,128)(2,1)} %bitcast.11, bf16[512,4608]{1,0:T(8,128)(2,1)} %bitcast.9, ...), custom_call_target="tpu_custom_call" | custom-call | tf_op jit(solution)/shard_map/pallas_call | solution.py:818
  30.2 0.7 %shard_map.105 = (f32[4,288]{1,0:T(4,128)}, bf16[2,4,8,2048]{3,2,1,0:T(8,128)(2,1)}) custom-call(f32[4,288]{1,0:T(4,128)S(1)} %get-tuple-element.6.out_ref, bf16[2,4,8,2048]{3,2,1,0:T(8,128)(2,1)S(1)} %get-tuple-element.7.dec_ref), custom_call_target="tpu_custom_call" | custom-call | tf_op jit(solution)/shard_map/pallas_call | solution.py:870
